TPU v7x, 256 devices: a 4x2x16 block of a 4x16x16 slice. The times are simulated.
256 devices in a mesh: group: 2 (over y), seq: 64 (over x, z), tensor: 2 (over core).
Axes of the slice: x: 4, y: 2, z: 16, core: 2. Of those that a mesh axis runs over, the one named last changes fastest.
The devices are a block of a 4x16x16 slice.
Arguments:
- query: bfloat16 [32, 64, 128], P('group', 'tensor'), parts along dimension 0, may hold values from -400 to 400
- key_cache: bfloat16 [4096, 128, 8, 128], P(('group', 'seq'), None, 'tensor'), parts along dimension 0, may hold values from -6 to 6
- value_cache: bfloat16 [4096, 128, 8, 128], P(('group', 'seq'), None, 'tensor'), parts along dimension 0, may hold values from -6 to 6
- lengths: int32 [32], P('group'), parts along dimension 0, may hold values from 1 to 32768, 129024 in all
- page_order: int32 [4096], P('group'), parts along dimension 0, may hold values from 0 to 2047, as said below
- out_weight: bfloat16 [8192, 8192], P('tensor', 'seq'), may hold values from -0.59765625 to 0.59765625
Outputs:
- mixed: bfloat16 [32, 8192], P(('group', 'tensor'), 'seq'), parts along dimension 0
There are 2 independent parts, one for each index of `group`. A program takes and returns all parts, laid end to end along the dimension named above; an argument that names none is the same for every part. Nothing has to cross between parts.
Inputs may be any that keep to these rules, and one draw needn't show every extreme that they name: The sequences' lengths sum to 129024; one equals 32768. `page_order`: a permutation of the pages.
All inputs are finite; a program needn't handle non-finite values.
Results may differ from a plain program's by a relative error of at most 0.0065.
Values may be sent and summed in bfloat16 or wider, within the bound.
A program may use at most 64 MiB of HBM per device.

v0:
```python
import math

import jax
import jax.numpy as jnp
from jax import lax
from jax.sharding import PartitionSpec as P


def sent_to_all(value, axis):
    peers = lax.axis_size(axis)
    return lax.all_to_all(
        jnp.broadcast_to(value[None], (peers, *value.shape)), axis, 0, 0, tiled=True
    )


def of_everyone(value, axis):
    return sent_to_all(value, axis).max(axis=0)


def of_everyone_2(value, axis):
    return sent_to_all(value, axis).sum(axis=0)


def cut_along(value, dim, peers):
    lengths = value.shape
    blocks = value.reshape(*lengths[:dim], peers, lengths[dim] // peers, *lengths[dim + 1 :])
    return jnp.moveaxis(blocks, dim, 0)


def sum_at_owner(value, axis, dim):
    peers = lax.axis_size(axis)
    blocks = lax.all_to_all(cut_along(value, dim, peers), axis, 0, 0, tiled=True)
    return jnp.sum(blocks, axis=0)


def in_order(blocks, dim):
    lengths = list(blocks.shape[1:])
    lengths[dim] *= blocks.shape[0]
    return jnp.moveaxis(blocks, 0, dim).reshape(lengths)


def gathered_copies(value, axis, dim):
    return in_order(sent_to_all(value, axis), dim)


def body(query, key_cache, value_cache, lengths, page_order, out_weight):
    pages_dev, page_len, kv_local, head_dim = key_cache.shape
    seq_count, heads_local = (query.shape[0], query.shape[1])
    group_size = heads_local // kv_local
    pool_size = page_order.shape[0]
    score_scale = 1.0 / math.sqrt(head_dim)
    counts = (lengths + page_len - 1) // page_len
    starts = jnp.cumsum(counts) - counts
    used_total = jnp.sum(counts)
    page_rank = (
        jnp.zeros((pool_size,), jnp.int32)
        .at[page_order]
        .set(jnp.arange(pool_size, dtype=jnp.int32))
    )
    first_page = lax.axis_index("seq") * pages_dev
    local_rank = lax.dynamic_slice_in_dim(page_rank, first_page, pages_dev)
    is_live = local_rank < used_total
    page_owner = jnp.sum((local_rank[:, None] >= starts[None, :]).astype(jnp.int32), axis=1) - 1
    page_owner = jnp.where(is_live, page_owner, -1)
    owner_safe = jnp.clip(page_owner, 0, seq_count - 1)
    block_index = local_rank - starts[owner_safe]
    positions = block_index[:, None] * page_len + jnp.arange(page_len, dtype=jnp.int32)[None, :]
    is_valid = is_live[:, None] & (positions < lengths[owner_safe][:, None])
    page_query = query[owner_safe].reshape(pages_dev, kv_local, group_size, head_dim)
    scores = (
        jnp.einsum("pghd,ptgd->pght", page_query, key_cache, preferred_element_type=jnp.float32)
        * score_scale
    )
    score_mask = is_valid[:, None, None, :]
    scores = jnp.where(score_mask, scores, -1e30)
    block_max = jnp.max(scores, axis=-1)
    weights = jnp.where(score_mask, jnp.exp(scores - block_max[..., None]), 0.0).astype(
        jnp.bfloat16
    )
    block_sum = jnp.sum(weights.astype(jnp.float32), axis=-1)
    block_out = jnp.einsum(
        "pght,ptgd->pghd", weights, value_cache, preferred_element_type=jnp.float32
    )
    flat_max = block_max.reshape(pages_dev, heads_local)
    onehot = page_owner[None, :] == jnp.arange(seq_count, dtype=jnp.int32)[:, None]
    seq_max = jnp.max(jnp.where(onehot[:, :, None], flat_max[None], -1e30), axis=1)
    factor = jnp.exp(flat_max - seq_max[owner_safe])
    onehot_wide = onehot.astype(jnp.float32)
    seq_sum = jnp.dot(
        onehot_wide,
        factor * block_sum.reshape(pages_dev, heads_local),
        precision=lax.Precision.HIGHEST,
    )
    scaled_out = (factor[:, :, None] * block_out.reshape(pages_dev, heads_local, head_dim)).reshape(
        pages_dev, heads_local * head_dim
    )
    seq_out = jnp.dot(onehot_wide, scaled_out, precision=lax.Precision.HIGHEST)
    largest = of_everyone(seq_max, "seq")
    rescale = jnp.exp(seq_max - largest)
    denominator = of_everyone_2(seq_sum * rescale, "seq")
    numerator = sum_at_owner(seq_out * jnp.repeat(rescale, head_dim, axis=1), "seq", 1)
    share_width = numerator.shape[1]
    share_start = lax.axis_index("seq") * share_width
    share_denominator = lax.dynamic_slice_in_dim(
        jnp.repeat(denominator, head_dim, axis=1), share_start, share_width, 1
    )
    attended_share = (numerator / share_denominator).astype(jnp.bfloat16)
    projected = jnp.dot(
        gathered_copies(attended_share, "seq", 1), out_weight, preferred_element_type=jnp.float32
    )
    return lax.psum_scatter(projected, "tensor", scatter_dimension=0, tiled=True).astype(
        jnp.bfloat16
    )


def solution(mesh):
    in_specs = (
        P("group", "tensor", None),
        P(("group", "seq"), None, "tensor", None),
        P(("group", "seq"), None, "tensor", None),
        P("group"),
        P("group"),
        P("tensor", "seq"),
    )
    out_specs = P(("group", "tensor"), "seq")
    return jax.shard_map(body, mesh=mesh, in_specs=in_specs, out_specs=out_specs, check_vma=False)
```

profile of v0, /device:TPU:40, one launch (start us, length us, event | category | flops | bytes accessed | tf_op | source)
XLA Modules:
  0.0 145.4 jit_solution(565332144684334216)
XLA Ops:
  0.0 1.4 fusion.21
  2.3 8.0 %scatter_custom_fusion = s32[2048]{0:T(1024)S(1)} fusion(s32[2048]{0:T(1024)S(1)} %compare_select_fusion, s32[2048]{0:T(1024)S(1)} %iota.19, s32[]{:T(128)} %constant.18.clone.1), kind=kCustom, calls=%fused_computation.36 | custom fusion | bytes 8196 | tf_op jit(solution)/shard_map/scatter | solution.py:58
  10.6 0.7 compare_select_fusion.1
  12.0 1.4 gather_fusion.1
  13.4 1.5 %gather_fusion.2 = bf16[32,32,128]{2,1,0:T(8,128)(2,1)S(1)} fusion(bf16[16,32,128]{2,1,0:T(8,128)(2,1)} %param.6, s32[1024]{0:T(1024)S(1)} %pad_clamp_fusion), kind=kCustom, calls=%fused_computation.2 | custom fusion | bytes 524416 | tf_op jit(solution)/shard_map/gather | solution.py:69
  15.0 4.6 %fusion.22 = (f32[32,4,8]{2,1,0:T(4,128)S(1)}, f32[32,4,8,128]{3,2,1,0:T(8,128)S(1)}) fusion(bf16[32,128,4,128]{3,2,1,0:T(4,128)(2,1)} %param.7, bf16[32,32,128]{2,1,0:T(8,128)(2,1)S(1)} %gather_fusion.2, pred[32,128]{1,0:T(8,128)(4,1)S(1)} %fusion.15), kind=kOutput, calls=%fused_computation.48 | convolution fusion | flops 33946624 | bytes 4988928 | tf_op jit(solution)/shard_map/pghd,ptgd->pght/dot_general | solution.py:71
  20.0 0.9 reshape.186
  20.9 29.0 %all-to-all-start = ((f32[64,1,512]{2,1,0:T(1,128)}), f32[64,1,512]{2,1,0:T(1,128)S(1)}, u32[]{:S(2)}, u32[]{:S(2)}) async-start(f32[64,1,512]{2,1,0:T(1,128)} %reshape.186), calls=%async_computation | async-start | bytes 262144 | tf_op jit(solution)/shard_map/all_to_all | solution.py:11
  51.1 13.7 %all-to-all-done = f32[64,1,512]{2,1,0:T(1,128)S(1)} async-done(((f32[64,1,512]{2,1,0:T(1,128)}), f32[64,1,512]{2,1,0:T(1,128)S(1)}, u32[]{:S(2)}, u32[]{:S(2)}) %all-to-all-start) | async-done | bytes 131104 | tf_op jit(solution)/shard_map/all_to_all | solution.py:11
  65.4 1.0 reduce.1
  66.8 0.9 reshape.190
  67.7 7.5 %all-to-all-start.2 = ((f32[64,1,512]{2,1,0:T(1,128)}), f32[64,1,512]{2,1,0:T(1,128)S(1)}, u32[]{:S(2)}, u32[]{:S(2)}) async-start(f32[64,1,512]{2,1,0:T(1,128)} %reshape.190), calls=%async_computation.2 | async-start | bytes 262144 | tf_op jit(solution)/shard_map/all_to_all | solution.py:11
  75.2 3.4 %fusion = f32[32,4,8,128]{3,2,1,0:T(8,128)S(1)} fusion(bf16[32,128,4,128]{3,2,1,0:T(4,128)(2,1)} %param.8, f32[32,4,8,128]{3,2,1,0:T(8,128)S(1)} %get-tuple-element.11, f32[32,4,8]{2,1,0:T(4,128)S(1)} %get-tuple-element.10, pred[32,128]{1,0:T(8,128)(4,1)S(1)} %fusion.15), kind=kOutput, calls=%fused_computation.6 | convolution fusion | flops 33947648 | bytes 5251072 | tf_op jit(solution)/shard_map/pght,ptgd->pghd/dot_general | solution.py:81
  79.0 1.1 convolution_multiply_fusion
  80.6 1.0 reshape.188
  81.6 8.5 %all-to-all-done.2 = f32[64,1,512]{2,1,0:T(1,128)S(1)} async-done(((f32[64,1,512]{2,1,0:T(1,128)}), f32[64,1,512]{2,1,0:T(1,128)S(1)}, u32[]{:S(2)}, u32[]{:S(2)}) %all-to-all-start.2) | async-done | bytes 131104 | tf_op jit(solution)/shard_map/all_to_all | solution.py:11
  90.2 7.7 %all-to-all-start.1 = ((f32[64,1,1024]{2,1,0:T(1,128)}), f32[64,1,1024]{2,1,0:T(1,128)S(1)}, u32[]{:S(2)}, u32[]{:S(2)}) async-start(f32[64,1,1024]{2,1,0:T(1,128)} %reshape.188), calls=%async_computation.1 | async-start | bytes 524288 | tf_op jit(solution)/shard_map/all_to_all | solution.py:32
  97.9 1.0 reduce.3
  99.4 17.0 %all-to-all-done.1 = f32[64,1,1024]{2,1,0:T(1,128)S(1)} async-done(((f32[64,1,1024]{2,1,0:T(1,128)}), f32[64,1,1024]{2,1,0:T(1,128)S(1)}, u32[]{:S(2)}, u32[]{:S(2)}) %all-to-all-start.1) | async-done | bytes 262176 | tf_op jit(solution)/shard_map/all_to_all | solution.py:32
  116.4 1.3 reduce.2
  118.0 0.8 reshape.192
  118.8 8.7 %all-to-all-start.3 = ((bf16[64,2,512]{2,1,0:T(2,128)(2,1)}), bf16[64,2,512]{2,1,0:T(2,128)(2,1)S(1)}, u32[]{:S(2)}, u32[]{:S(2)}) async-start(bf16[64,2,512]{2,1,0:T(2,128)(2,1)} %reshape.192), calls=%async_computation.3 | async-start | bytes 262144 | tf_op jit(solution)/shard_map/all_to_all | solution.py:11
  128.7 12.7 %all-to-all-done.3 = bf16[64,2,512]{2,1,0:T(2,128)(2,1)S(1)} async-done(((bf16[64,2,512]{2,1,0:T(2,128)(2,1)}), bf16[64,2,512]{2,1,0:T(2,128)(2,1)S(1)}, u32[]{:S(2)}, u32[]{:S(2)}) %all-to-all-start.3) | async-done | bytes 131104 | tf_op jit(solution)/shard_map/all_to_all | solution.py:11
  142.2 2.5 %all-reduce = bf16[16,128]{1,0:T(8,128)(2,1)S(1)} all-reduce(f32[16,128]{1,0:T(8,128)S(1)} %fusion.23), channel_id=2, replica_groups=mesh['group'=2,'seq'=64,'tensor'=2] {'tensor'}, use_global_device_ids=true, to_apply=%region_10.11.clone | all-reduce | flops 2048 | bytes 12288
  (50 shorter events, 8.2 us)
Async XLA Ops:
  0.0 142.0 %copy-start = (bf16[4096,128]{1,0:T(8,128)(2,1)S(1)}, bf16[4096,128]{1,0:T(8,128)(2,1)}, u32[]{:S(2)}) copy-start(bf16[4096,128]{1,0:T(8,128)(2,1)} %param.11) | copy-start | bytes 3145732
  20.9 44.0 %all-to-all-start = ((f32[64,1,512]{2,1,0:T(1,128)}), f32[64,1,512]{2,1,0:T(1,128)S(1)}, u32[]{:S(2)}, u32[]{:S(2)}) async-start(f32[64,1,512]{2,1,0:T(1,128)} %reshape.186), calls=%async_computation | async-start | bytes 262144 | tf_op jit(solution)/shard_map/all_to_all | solution.py:11
  67.7 22.5 %all-to-all-start.2 = ((f32[64,1,512]{2,1,0:T(1,128)}), f32[64,1,512]{2,1,0:T(1,128)S(1)}, u32[]{:S(2)}, u32[]{:S(2)}) async-start(f32[64,1,512]{2,1,0:T(1,128)} %reshape.190), calls=%async_computation.2 | async-start | bytes 262144 | tf_op jit(solution)/shard_map/all_to_all | solution.py:11
  80.1 47.4 %copy-start.1 = (u32[256]{0:T(256)S(1)}, u32[256]{0:T(256)}, u32[]{:S(2)}) copy-start(u32[256]{0:T(256)} %constant.62) | copy-start | bytes 3076
  90.2 26.2 %all-to-all-start.1 = ((f32[64,1,1024]{2,1,0:T(1,128)}), f32[64,1,1024]{2,1,0:T(1,128)S(1)}, u32[]{:S(2)}, u32[]{:S(2)}) async-start(f32[64,1,1024]{2,1,0:T(1,128)} %reshape.188), calls=%async_computation.1 | async-start | bytes 524288 | tf_op jit(solution)/shard_map/all_to_all | solution.py:32
  118.8 22.6 %all-to-all-start.3 = ((bf16[64,2,512]{2,1,0:T(2,128)(2,1)}), bf16[64,2,512]{2,1,0:T(2,128)(2,1)S(1)}, u32[]{:S(2)}, u32[]{:S(2)}) async-start(bf16[64,2,512]{2,1,0:T(2,128)(2,1)} %reshape.192), calls=%async_computation.3 | async-start | bytes 262144 | tf_op jit(solution)/shard_map/all_to_all | solution.py:11
where the time goes:
time: 147 us; the launch traced here: 145 us
  starting transfers between devices  52.9 us (36%)
  waiting for transfers between devices  51.9 us (35%)
  local copies, waits for them, and re-layouts  20.3 us (14%)
  matrix products  9.43 us (6%)
  other arithmetic  7.37 us (5%)
  blocking collectives  2.55 us (2%)
    all_to_all x3, starting transfers between devices, sent_to_all(): lax.all_to_all(jnp.broadcast_to(value[None], (peers, *value.shape)), axis...  45.2 us
    all_to_all x3, waiting for transfers between devices, sent_to_all(): lax.all_to_all(jnp.broadcast_to(value[None], (peers, *value.shape)), axis...  34.9 us
    all_to_all x1, waiting for transfers between devices, sum_at_owner(): lax.all_to_all(cut_along(value, dim, peers), axis, 0, 0, tiled=True)  17 us
    scatter x1, local copies, waits for them, and re-layouts, body(): page_rank = jnp.zeros((pool_size,), jnp.int32).at[page_order].set(jnp.ara...  8.04 us
    all_to_all x1, starting transfers between devices, sum_at_owner(): lax.all_to_all(cut_along(value, dim, peers), axis, 0, 0, tiled=True)  7.69 us
    unnamed x14, local copies, waits for them, and re-layouts  5.09 us
    dot_general x1, matrix products, body(): jnp.einsum('pghd,ptgd->pght', page_query, key_cache, preferred_element_ty...  4.57 us
    dot_general x1, matrix products, body(): jnp.einsum('pght,ptgd->pghd', weights, value_cache, preferred_element_typ...  3.44 us
  transfers between devices with their start and end apart: 4, of which 4 were waited for; matrix products, arithmetic and copies ran while one was open for 7% of the time, Pallas kernels for 0%

commit v1 on v0

v1 whole, which is shorter than its diff:
```python
import functools
import math

import jax
import jax.numpy as jnp
from jax import lax
from jax.experimental import pallas as pl
from jax.experimental.pallas import tpu as pltpu
from jax.sharding import PartitionSpec as P

MESH = pl.DeviceIdType.MESH
F32 = jnp.float32
BF16 = jnp.bfloat16
I32 = jnp.int32
LANES = 128
NEG = -1e30
PAGES_PER_STEP = 8


def kernel(
    dims,
    len_s, q_hbm, k_hbm, v_hbm, po_hbm, w_hbm, out_ref,
    q_v, k_v, v_v, po_v, w_v, val_v, meta_v, meta_s, cmod_v,
    mrun, lrun, orun, ofin,
    s1o, s1m, r1o, r1m, s2o, s2m, r2o, r2m, g_v, acc_v,
    q_sem, k_sem, v_sem, po_sem, w_sem, meta_sem,
    ws_sem, wr_sem, s1s_sem, s1r_sem, s1ms_sem, s1mr_sem,
    s2s_sem, s2r_sem, s2ms_sem, s2mr_sem, gzs_sem, gzr_sem, gxs_sem, gxr_sem,
):
    nx, nz, pages, page_len, kvh, ns, hl, hd, cores = dims
    rows = page_len * kvh
    hq = hl // nx
    sb = ns // cores
    group_size = hl // kvh
    scale = math.log2(math.e) / math.sqrt(hd)
    me = lax.axis_index("seq")
    t = lax.axis_index("tensor")
    x = me // nz
    z = me % nz
    steps = pages // PAGES_PER_STEP

    xpeers = []
    for dx in range(nx):
        for dt in range(cores):
            if dx or dt:
                xpeers.append(((x + dx) % nx, (t + dt) % cores))
    order = []
    for d in range(nz // 2, 0, -1):
        order.append(d)
        if d != nz - d:
            order.append(nz - d)

    def at(px, pz, pt):
        return {"seq": px * nz + pz, "tensor": pt}

    barrier = pltpu.get_barrier_semaphore()
    for px, pt in xpeers:
        pl.semaphore_signal(barrier, inc=1, device_id=at(px, z, pt), device_id_type=MESH)
    for d in order:
        pl.semaphore_signal(barrier, inc=1, device_id=at(x, (z + d) % nz, t), device_id_type=MESH)

    po_copy = pltpu.make_async_copy(po_hbm, po_v, po_sem)
    po_copy.start()
    q_copy = pltpu.make_async_copy(q_hbm, q_v, q_sem)
    q_copy.start()
    step_rows = PAGES_PER_STEP * rows

    def kv_copy(src, dst, sem, c):
        part = pl.ds(c * step_rows, step_rows)
        return pltpu.make_async_copy(src.at[part], dst.at[part], sem.at[c])

    for c in range(steps):
        kv_copy(k_hbm, k_v, k_sem, c).start()
        kv_copy(v_hbm, v_v, v_sem, c).start()
    w_copy = pltpu.make_async_copy(w_hbm, w_v.at[t], w_sem)
    w_copy.start()

    lens = [len_s[s] for s in range(ns)]
    starts = []
    run = jnp.int32(0)
    for s in range(ns):
        starts.append(run)
        run = run + lax.shift_right_logical(lens[s] + (page_len - 1), int(math.log2(page_len)))
    pr = po_v.shape[0]
    rank = lax.broadcasted_iota(I32, (pr, LANES), 0) * LANES + lax.broadcasted_iota(I32, (pr, LANES), 1)
    owner = jnp.zeros((pr, LANES), I32)
    end = jnp.full((pr, LANES), lens[0], I32)
    for s in range(1, ns):
        past = rank >= starts[s]
        owner = jnp.where(past, s, owner)
        end = jnp.where(past, lens[s] + starts[s] * page_len, end)
    valid = jnp.clip(end - rank * page_len, 0, page_len)
    owner = jnp.where(valid > 0, owner, ns)
    val_v[...] = (owner * 256 + valid).astype(F32)

    cl = lax.broadcasted_iota(I32, (hl, rows), 1)
    hr = lax.broadcasted_iota(I32, (hl, rows), 0)
    cmod_v[...] = jnp.where(cl % kvh == hr // group_size, cl, 1 << 20)
    mrun[0] = jnp.full((hl, LANES), NEG, F32)
    lrun[0] = jnp.zeros((hl, LANES), F32)
    orun[0] = jnp.zeros((hl, hd), F32)

    po_copy.wait()
    ids = lax.broadcasted_iota(I32, (pages, LANES), 0) + me * pages
    acc = jnp.zeros((pages, LANES), F32)
    for i in range(pr):
        hit = jnp.broadcast_to(po_v[i : i + 1, :], (pages, LANES)) == ids
        acc = acc + jnp.where(hit, jnp.broadcast_to(val_v[i : i + 1, :], (pages, LANES)), 0.0)
    val_col = jnp.broadcast_to(jnp.sum(acc, axis=1, keepdims=True), (pages, LANES))
    pad = jnp.concatenate([val_col, jnp.zeros((LANES - pages, LANES), F32)], axis=0)
    val_row = jnp.transpose(pad)[0:1, :]
    own_col = lax.shift_right_logical(val_col.astype(I32), 8)
    val_row_i = val_row.astype(I32)
    own_row = lax.shift_right_logical(val_row_i, 8)
    prow = lax.broadcasted_iota(I32, (pages, LANES), 0)
    lane = lax.broadcasted_iota(I32, (pages, LANES), 1)
    same = (own_col == jnp.broadcast_to(own_row, (pages, LANES))) & (prow < lane)
    prev = jnp.max(jnp.where(same, (prow + 1).astype(F32), 0.0), axis=0, keepdims=True).astype(I32)
    last = jnp.max(jnp.where(own_col == lane, (prow + 1).astype(F32), 0.0), axis=0, keepdims=True).astype(I32)
    meta_v[0:1, :] = prev * 8192 + val_row_i
    meta_v[1:2, :] = last
    meta_copy = pltpu.make_async_copy(meta_v, meta_s, meta_sem)
    meta_copy.start()
    meta_copy.wait()
    q_copy.wait()

    def step(c, carry):
        kv_copy(k_hbm, k_v, k_sem, c).wait()
        kv_copy(v_hbm, v_v, v_sem, c).wait()
        for i in range(PAGES_PER_STEP):
            p = c * PAGES_PER_STEP + i
            code = meta_s[0, p]
            nvalid = jnp.bitwise_and(code, 255) * kvh
            own = jnp.minimum(jnp.bitwise_and(lax.shift_right_logical(code, 8), 31), ns - 1)
            before = jnp.clip(lax.shift_right_logical(code, 13), 0, pages)
            part = pl.ds(pl.multiple_of(p * rows, rows), rows)
            sc = lax.dot_general(q_v[own], k_v[part, :], (((1,), (1,)), ((), ())), preferred_element_type=F32)
            sc = jnp.where(cmod_v[...] < nvalid, sc, NEG)
            top = jnp.max(sc, axis=1, keepdims=True)
            wt = jnp.exp2((sc - top) * scale)
            tot = jnp.sum(wt, axis=1, keepdims=True)
            o = jnp.dot(wt.astype(BF16), v_v[part, :], preferred_element_type=F32)
            mp = mrun[before]
            mb = jnp.broadcast_to(top, (hl, LANES))
            mn = jnp.maximum(mp, mb)
            fa = jnp.exp2((mp - mn) * scale)
            fb = jnp.exp2((mb - mn) * scale)
            mrun[p + 1] = mn
            lrun[p + 1] = fa * lrun[before] + fb * jnp.broadcast_to(tot, (hl, LANES))
            orun[p + 1] = fa * orun[before] + fb * o
        return carry

    lax.fori_loop(0, steps, step, 0)

    lane_h = lax.broadcasted_iota(I32, (hl, LANES), 1)
    mpack = jnp.zeros((hl, LANES), F32)
    lpack = jnp.zeros((hl, LANES), F32)
    for s in range(ns):
        f = jnp.clip(meta_s[1, s], 0, pages)
        ofin[s] = orun[f]
        mpack = jnp.where(lane_h == s, mrun[f], mpack)
        lpack = jnp.where(lane_h == s, lrun[f], lpack)
    both = jnp.concatenate([mpack, lpack, jnp.zeros((LANES - 2 * hl, LANES), F32)], axis=0)
    mlt = jnp.transpose(both)[0:ns, :]
    for ct in range(cores):
        part = mlt[ct * sb : (ct + 1) * sb, :]
        for cx in range(nx):
            s1m[ct, cx] = part if cx == 0 else pltpu.roll(part, LANES - cx * hq, 1)
            for j in range(hq):
                s1o[ct, cx, j] = ofin[ct * sb : (ct + 1) * sb, cx * hq + j, :].astype(BF16)
    r1o[t, x] = s1o[t, x]
    r1m[t, x] = s1m[t, x]

    pl.semaphore_wait(barrier, len(xpeers) + len(order))

    def s1_copies(i, px, pt):
        o = pltpu.make_async_remote_copy(
            src_ref=s1o.at[pt, px], dst_ref=r1o.at[t, x], send_sem=s1s_sem.at[i], recv_sem=s1r_sem.at[t, x],
            device_id=at(px, z, pt), device_id_type=MESH)
        m = pltpu.make_async_remote_copy(
            src_ref=s1m.at[pt, px], dst_ref=r1m.at[t, x], send_sem=s1ms_sem.at[i], recv_sem=s1mr_sem.at[t, x],
            device_id=at(px, z, pt), device_id_type=MESH)
        return m, o

    def s1_arrivals(px, pt):
        o = pltpu.make_async_remote_copy(
            src_ref=s1o.at[pt, px], dst_ref=r1o.at[pt, px], send_sem=s1s_sem.at[0], recv_sem=s1r_sem.at[pt, px],
            device_id=at(px, z, pt), device_id_type=MESH)
        m = pltpu.make_async_remote_copy(
            src_ref=s1m.at[pt, px], dst_ref=r1m.at[pt, px], send_sem=s1ms_sem.at[0], recv_sem=s1mr_sem.at[pt, px],
            device_id=at(px, z, pt), device_id_type=MESH)
        return m, o

    for i, (px, pt) in enumerate(xpeers):
        for copy in s1_copies(i, px, pt):
            copy.start()

    w_copy.wait()
    w_send = pltpu.make_async_remote_copy(
        src_ref=w_v.at[t], dst_ref=w_v.at[t], send_sem=ws_sem, recv_sem=wr_sem,
        device_id=at(x, z, (t + 1) % cores), device_id_type=MESH)
    w_recv = pltpu.make_async_remote_copy(
        src_ref=w_v.at[t], dst_ref=w_v.at[(t + 1) % cores], send_sem=ws_sem, recv_sem=wr_sem,
        device_id=at(x, z, (t + 1) % cores), device_id_type=MESH)
    w_send.start()

    for px, pt in xpeers:
        for copy in s1_arrivals(px, pt):
            copy.wait_recv()

    lane_s = lax.broadcasted_iota(I32, (sb, LANES), 1)
    tops, sums = [], []
    for ct in range(cores):
        ml = [r1m[ct, cx] for cx in range(nx)]
        top = functools.reduce(jnp.maximum, ml)
        fs = [jnp.exp2((m - top) * scale) for m in ml]
        tot = functools.reduce(jnp.add, [f * pltpu.roll(m, LANES - hl, 1) for f, m in zip(fs, ml)])
        tops.append(top)
        sums.append(tot)
        for j in range(hq):
            num = functools.reduce(
                jnp.add,
                [jnp.broadcast_to(fs[cx][:, j : j + 1], (sb, hd)) * r1o[ct, cx, j].astype(F32) for cx in range(nx)])
            s2o[ct * hq + j] = num.astype(BF16)
    mm = jnp.where(lane_s < hq, tops[0], pltpu.roll(tops[1], hq, 1))
    ll = jnp.where(lane_s < hq, sums[0], pltpu.roll(sums[1], hq, 1))
    both = jnp.concatenate([mm, ll, jnp.zeros((LANES - 2 * sb, LANES), F32)], axis=0)
    s2m[...] = jnp.transpose(both)[0:nz, :].reshape(nz, 1, LANES)
    r2o[z] = s2o[z]
    r2m[z] = s2m[z]

    def s2_copies(d, dst_z, src_z, slot_z):
        o = pltpu.make_async_remote_copy(
            src_ref=s2o.at[dst_z], dst_ref=r2o.at[slot_z], send_sem=s2s_sem.at[d], recv_sem=s2r_sem.at[slot_z],
            device_id=at(x, dst_z, t), device_id_type=MESH)
        m = pltpu.make_async_remote_copy(
            src_ref=s2m.at[dst_z], dst_ref=r2m.at[slot_z], send_sem=s2ms_sem.at[d], recv_sem=s2mr_sem.at[slot_z],
            device_id=at(x, dst_z, t), device_id_type=MESH)
        return m, o

    for d in order:
        for copy in s2_copies(d, (z + d) % nz, z, z):
            copy.start()
    for d in reversed(order):
        pz = (z + d) % nz
        for copy in s2_copies(d, pz, pz, pz):
            copy.wait_recv()

    ml = r2m[...].reshape(nz, LANES)
    top = jnp.max(ml, axis=0, keepdims=True)
    f = jnp.exp2((ml - top) * scale)
    den = jnp.sum(f * pltpu.roll(ml, LANES - sb, 1), axis=0, keepdims=True)
    lane_z = lax.broadcasted_iota(I32, (nz, LANES), 1)
    f = jnp.where(lane_z < sb, f / den, 0.0)
    ft = jnp.transpose(jnp.concatenate([f, jnp.zeros((LANES - nz, LANES), F32)], axis=0))[0:sb, :]
    att = functools.reduce(
        jnp.add, [jnp.broadcast_to(ft[:, i : i + 1], (sb, hd)) * r2o[i].astype(F32) for i in range(nz)])
    g_v[x, z] = att.astype(BF16)

    def gz_copy(d, pz, slot):
        return pltpu.make_async_remote_copy(
            src_ref=g_v.at[x, z], dst_ref=g_v.at[x, slot], send_sem=gzs_sem.at[d], recv_sem=gzr_sem.at[slot],
            device_id=at(x, pz, t), device_id_type=MESH)

    def gx_copy(dx, slot_x, slot):
        return pltpu.make_async_remote_copy(
            src_ref=g_v.at[x, slot], dst_ref=g_v.at[slot_x, slot], send_sem=gxs_sem.at[dx, slot],
            recv_sem=gxr_sem.at[slot_x, slot], device_id=at((x + dx) % nx, z, t), device_id_type=MESH)

    for d in order:
        gz_copy(d, (z + d) % nz, z).start()
    for dx in range(1, nx):
        gx_copy(dx, x, z).start()
    for d in reversed(order):
        pz = (z + d) % nz
        gz_copy(d, pz, pz).wait_recv()
        for dx in range(1, nx):
            gx_copy(dx, x, pz).start()
    w_recv.wait_recv()
    for dx in range(1, nx):
        for d in range(nz):
            gx_copy(dx, (x + dx) % nx, d).wait_recv()

    out = jnp.zeros((sb, hd), F32)
    for ct in range(cores):
        for cx in range(nx):
            for j in range(0, hq, 2):
                lhs = jnp.concatenate([g_v[cx, ct * hq + j], g_v[cx, ct * hq + j + 1]], axis=1)
                first = (cx * hq + j) * hd
                out = out + jnp.dot(lhs, w_v[ct, first : first + 2 * hd, :], preferred_element_type=F32)
    out_ref[...] = out.astype(out_ref.dtype)

    w_send.wait_send()
    for i, (px, pt) in enumerate(xpeers):
        for copy in s1_copies(i, px, pt):
            copy.wait_send()
    for d in order:
        for copy in s2_copies(d, (z + d) % nz, z, z):
            copy.wait_send()
        gz_copy(d, (z + d) % nz, z).wait_send()
    for dx in range(1, nx):
        for d in range(nz):
            gx_copy(dx, x, d).wait_send()


def body(query, key_cache, value_cache, lengths, page_order, out_weight):
    pages, page_len, kvh, hd = key_cache.shape
    ns, hl = query.shape[0], query.shape[1]
    cores = lax.axis_size("tensor")
    nz = ns
    nx = lax.axis_size("seq") // nz
    hq = hl // nx
    sb = ns // cores
    rows = page_len * kvh
    pr = page_order.shape[0] // LANES
    wr, wc = out_weight.shape
    dims = (nx, nz, pages, page_len, kvh, ns, hl, hd, cores)
    steps = pages // PAGES_PER_STEP
    nxp = nx * cores - 1
    dma = pltpu.SemaphoreType.DMA
    return pl.pallas_call(
        functools.partial(kernel, dims),
        out_shape=jax.ShapeDtypeStruct((sb, wc), BF16),
        in_specs=[pl.BlockSpec(memory_space=pltpu.SMEM)] + [pl.BlockSpec(memory_space=pl.ANY)] * 5,
        out_specs=pl.BlockSpec(memory_space=pltpu.VMEM),
        scratch_shapes=[
            pltpu.VMEM((ns, hl, hd), BF16),
            pltpu.VMEM((pages * rows, hd), BF16),
            pltpu.VMEM((pages * rows, hd), BF16),
            pltpu.VMEM((pr, LANES), I32),
            pltpu.VMEM((cores, wr, wc), BF16),
            pltpu.VMEM((pr, LANES), F32),
            pltpu.VMEM((8, LANES), I32),
            pltpu.SMEM((8, LANES), I32),
            pltpu.VMEM((hl, rows), I32),
            pltpu.VMEM((pages + 1, hl, LANES), F32),
            pltpu.VMEM((pages + 1, hl, LANES), F32),
            pltpu.VMEM((pages + 1, hl, hd), F32),
            pltpu.VMEM((ns, hl, hd), F32),
            pltpu.VMEM((cores, nx, hq, sb, hd), BF16),
            pltpu.VMEM((cores, nx, sb, LANES), F32),
            pltpu.VMEM((cores, nx, hq, sb, hd), BF16),
            pltpu.VMEM((cores, nx, sb, LANES), F32),
            pltpu.VMEM((nz, sb, hd), BF16),
            pltpu.VMEM((nz, 1, LANES), F32),
            pltpu.VMEM((nz, sb, hd), BF16),
            pltpu.VMEM((nz, 1, LANES), F32),
            pltpu.VMEM((nx, nz, sb, hd), BF16),
            pltpu.VMEM((sb, LANES), F32),
            dma, dma((steps,)), dma((steps,)), dma, dma, dma,
            dma, dma, dma((nxp,)), dma((cores, nx)), dma((nxp,)), dma((cores, nx)),
            dma((nz,)), dma((nz,)), dma((nz,)), dma((nz,)), dma((nz,)), dma((nz,)), dma((nx, nz)), dma((nx, nz)),
        ],
        compiler_params=pltpu.CompilerParams(collective_id=0, has_side_effects=True),
        name="paged_decode",
    )(
        lengths, query, key_cache.reshape(pages * rows, hd), value_cache.reshape(pages * rows, hd),
        page_order.reshape(pr, LANES), out_weight)


def solution(mesh):
    in_specs = (
        P("group", "tensor", None),
        P(("group", "seq"), None, "tensor", None),
        P(("group", "seq"), None, "tensor", None),
        P("group"),
        P("group"),
        P("tensor", "seq"),
    )
    out_specs = P(("group", "tensor"), "seq")
    return jax.shard_map(body, mesh=mesh, in_specs=in_specs, out_specs=out_specs, check_vma=False)
```

time: 147 us -> 61.2 us (0.42); the launches traced: 145 us -> 61.1 us
  Pallas kernels: 0 us -> 59.8 us
  starting transfers between devices: 52.9 us -> 0 us
  waiting for transfers between devices: 51.9 us -> 0 us
  local copies, waits for them, and re-layouts: 20.3 us -> 1.26 us
  matrix products: 9.43 us -> 0 us
  other arithmetic: 7.37 us -> 0 us
  blocking collectives: 2.55 us -> 0 us
    pallas_call x0 -> x1, Pallas kernels: none -> 59.8 us  [body(): pl.pallas_call(functools.partial(kernel, dims), out_shape=jax.ShapeDtypeS...]
    all_to_all x4 -> x0, starting transfers between devices: 52.9 us -> none  [the longest x3 45.2 us: sent_to_all(): lax.all_to_all(jnp.broadcast_to(value[None], (peers, *value.shape)), axis...]
    all_to_all x4 -> x0, waiting for transfers between devices: 51.9 us -> none  [the longest x3 34.9 us: sent_to_all(): lax.all_to_all(jnp.broadcast_to(value[None], (peers, *value.shape)), axis...]
    dot_general x5 -> x0, matrix products: 9.43 us -> none  [the longest x1 4.57 us: body(): jnp.einsum('pghd,ptgd->pght', page_query, key_cache, preferred_element_ty...]
    scatter x1 -> x0, local copies, waits for them, and re-layouts: 8.04 us -> none  [body(): page_rank = jnp.zeros((pool_size,), jnp.int32).at[page_order].set(jnp.ara...]
    gather x4 -> x0, local copies, waits for them, and re-layouts: 4.14 us -> none  [the longest x1 1.51 us: body(): query[owner_safe].reshape(pages_dev, kv_local, group_size, head_dim)]
    unnamed x14 -> x1, local copies, waits for them, and re-layouts: 5.09 us -> 1.26 us
    all_to_all x3 -> x0, other arithmetic: 3.16 us -> none  [the longest x2 1.9 us: sent_to_all(): lax.all_to_all(jnp.broadcast_to(value[None], (peers, *value.shape)), axis...]
  transfers between devices with their start and end apart: 4 -> 0, of which waited for: 4 -> 0; matrix products, arithmetic and copies ran while one was open for 7% -> 0% of each run, Pallas kernels for 0% -> 0%
where the time goes in v1:
time: 61.2 us; the launch traced here: 61.1 us
  Pallas kernels  59.8 us (98%)
  local copies, waits for them, and re-layouts  1.26 us (2%)
    pallas_call x1, Pallas kernels, body(): pl.pallas_call(functools.partial(kernel, dims), out_shape=jax.ShapeDtypeS...  59.8 us
    unnamed x1, local copies, waits for them, and re-layouts  1.26 us

profile of v1, /device:TPU:40, one launch (start us, length us, event | category | flops | bytes accessed | tf_op | source)
XLA Modules:
  0.0 61.1 jit_solution(12530309516829870961)
XLA Ops:
  0.0 59.8 %paged_decode.1 = bf16[8,128]{1,0:T(8,128)(2,1)} custom-call(s32[16]{0:T(128)} %len_s.1, bf16[16,32,128]{2,1,0:T(8,128)(2,1)} %q_hbm.1, bf16[16384,128]{1,0:T(8,128)(2,1)} %bitcast.3, bf16[16384,128]{1,0:T(8,128)(2,1)} %bitcast.4, s32[16,128]{1,0:T(8,128)} %bitcast.5, bf16[4096,128]{1,0:T(8,128)(2,1)} %w_hbm.1), custom_call_target="tpu_custom_call" | custom-call | tf_op jit(solution)/shard_map/paged_decode/pallas_call | solution.py:321
  59.8 1.3 %copy.8 = bf16[8,128]{1,0:T(8,128)(2,1)} copy(bf16[8,128]{1,0:T(8,128)(2,1)} %paged_decode.1) | data formatting | bytes 4096

commit v2 on v1

v2 whole, which is shorter than its diff:
```python
import functools
import math

import jax
import jax.numpy as jnp
from jax import lax
from jax.experimental import pallas as pl
from jax.experimental.pallas import tpu as pltpu
from jax.sharding import PartitionSpec as P

MESH = pl.DeviceIdType.MESH
F32 = jnp.float32
BF16 = jnp.bfloat16
I32 = jnp.int32
LANES = 128
NEG = -1e30
PAGES_PER_STEP = 8


def kernel(
    dims,
    len_s, q_hbm, k_hbm, v_hbm, po_hbm, w_hbm, out_ref,
    q_v, k_v, v_v, po_v, w_v, val_v, meta_v, meta_s, cmod_v,
    wt_v, mtop, ltot, mrun, lrun, orun, ofin,
    s1o, s1m, r1o, r1m, s2o, s2m, r2o, r2m, g_v,
    q_sem, k_sem, v_sem, po_sem, w_sem, meta_sem,
    ws_sem, wr_sem, s1s_sem, s1r_sem, s1ms_sem, s1mr_sem,
    s2s_sem, s2r_sem, s2ms_sem, s2mr_sem, gd_sem, gz_sem, gx_sem, gr_sem,
):
    nx, nz, pages, page_len, kvh, ns, hl, hd, cores = dims
    rows = page_len * kvh
    hq = hl // nx
    sb = ns // cores
    group_size = hl // kvh
    scale = math.log2(math.e) / math.sqrt(hd)
    me = lax.axis_index("seq")
    t = lax.axis_index("tensor")
    x = me // nz
    z = me % nz
    steps = pages // PAGES_PER_STEP
    spots = (nz - 1, 0)

    def at(px, pz, pt):
        return {"seq": px * nz + pz, "tensor": pt}

    def remote(src, dst, send, recv, to):
        return pltpu.make_async_remote_copy(
            src_ref=src, dst_ref=dst, send_sem=send, recv_sem=recv, device_id=to, device_id_type=MESH)

    po_copy = pltpu.make_async_copy(po_hbm, po_v, po_sem)
    po_copy.start()
    q_copy = pltpu.make_async_copy(q_hbm, q_v, q_sem)
    q_copy.start()
    step_rows = PAGES_PER_STEP * rows

    def kv_copy(src, dst, sem, c):
        part = pl.ds(c * step_rows, step_rows)
        return pltpu.make_async_copy(src.at[part], dst.at[part], sem.at[c])

    for c in range(steps):
        kv_copy(k_hbm, k_v, k_sem, c).start()
    for c in range(steps):
        kv_copy(v_hbm, v_v, v_sem, c).start()
    w_copy = pltpu.make_async_copy(w_hbm, w_v.at[t], w_sem)
    w_copy.start()

    xpeers = []
    for dx in range(nx):
        for dt in range(cores):
            if dx or dt:
                xpeers.append(((x + dx) % nx, (t + dt) % cores))
    is_spot = (z == spots[0]) | (z == spots[1])
    barrier = pltpu.get_barrier_semaphore()

    def greet(px, pz, pt):
        pl.semaphore_signal(barrier, inc=1, device_id=at(px, pz, pt), device_id_type=MESH)

    for px, pt in xpeers:
        greet(px, z, pt)
    for o in range(cores):
        @pl.when(z != spots[o])
        def _():
            greet(x, spots[o], t)

        @pl.when(z == spots[o])
        def _():
            for pz in range(nz):
                if pz not in spots:
                    greet(x, pz, t)
            for dx in range(1, nx):
                greet((x + dx) % nx, spots[1 - o], t)

    lens = [len_s[s] for s in range(ns)]
    starts = []
    run = jnp.int32(0)
    for s in range(ns):
        starts.append(run)
        run = run + lax.shift_right_logical(lens[s] + (page_len - 1), int(math.log2(page_len)))
    pr = po_v.shape[0]
    rank = lax.broadcasted_iota(I32, (pr, LANES), 0) * LANES + lax.broadcasted_iota(I32, (pr, LANES), 1)
    owner = jnp.zeros((pr, LANES), I32)
    end = jnp.full((pr, LANES), lens[0], I32)
    for s in range(1, ns):
        past = rank >= starts[s]
        owner = jnp.where(past, s, owner)
        end = jnp.where(past, lens[s] + starts[s] * page_len, end)
    valid = jnp.clip(end - rank * page_len, 0, page_len)
    owner = jnp.where(valid > 0, owner, ns)
    val_v[...] = (owner * 256 + valid).astype(F32)

    cl = lax.broadcasted_iota(I32, (hl, rows), 1)
    hr = lax.broadcasted_iota(I32, (hl, rows), 0)
    cmod_v[...] = jnp.where(cl % kvh == hr // group_size, cl, 1 << 20)
    mrun[0] = jnp.full((hl, LANES), NEG, F32)
    lrun[0] = jnp.zeros((hl, LANES), F32)
    orun[0] = jnp.zeros((hl, hd), F32)

    po_copy.wait()
    ids = lax.broadcasted_iota(I32, (pages, LANES), 0) + me * pages
    acc = jnp.zeros((pages, LANES), F32)
    for i in range(pr):
        hit = jnp.broadcast_to(po_v[i : i + 1, :], (pages, LANES)) == ids
        acc = acc + jnp.where(hit, jnp.broadcast_to(val_v[i : i + 1, :], (pages, LANES)), 0.0)
    val_col = jnp.broadcast_to(jnp.sum(acc, axis=1, keepdims=True), (pages, LANES))
    pad = jnp.concatenate([val_col, jnp.zeros((LANES - pages, LANES), F32)], axis=0)
    val_row = jnp.transpose(pad)[0:1, :]
    own_col = lax.shift_right_logical(val_col.astype(I32), 8)
    val_row_i = val_row.astype(I32)
    own_row = lax.shift_right_logical(val_row_i, 8)
    prow = lax.broadcasted_iota(I32, (pages, LANES), 0)
    lane = lax.broadcasted_iota(I32, (pages, LANES), 1)
    same = (own_col == jnp.broadcast_to(own_row, (pages, LANES))) & (prow < lane)
    prev = jnp.max(jnp.where(same, (prow + 1).astype(F32), 0.0), axis=0, keepdims=True).astype(I32)
    last = jnp.max(jnp.where(own_col == lane, (prow + 1).astype(F32), 0.0), axis=0, keepdims=True).astype(I32)
    meta_v[0:1, :] = prev * 8192 + val_row_i
    meta_v[1:2, :] = last
    meta_copy = pltpu.make_async_copy(meta_v, meta_s, meta_sem)
    meta_copy.start()
    meta_copy.wait()
    q_copy.wait()

    def page_part(p):
        return pl.ds(pl.multiple_of(p * rows, rows), rows)

    def score_step(c, carry):
        kv_copy(k_hbm, k_v, k_sem, c).wait()
        for i in range(PAGES_PER_STEP):
            p = c * PAGES_PER_STEP + i
            code = meta_s[0, p]
            nvalid = jnp.bitwise_and(code, 255) * kvh
            own = jnp.minimum(jnp.bitwise_and(lax.shift_right_logical(code, 8), 31), ns - 1)
            before = jnp.clip(lax.shift_right_logical(code, 13), 0, pages)
            sc = lax.dot_general(
                q_v[own], k_v[page_part(p), :], (((1,), (1,)), ((), ())), preferred_element_type=F32)
            sc = jnp.where(cmod_v[...] < nvalid, sc, NEG)
            top = jnp.max(sc, axis=1, keepdims=True)
            wt = jnp.exp2((sc - top) * scale)
            wt_v[p] = wt.astype(BF16)
            top = jnp.broadcast_to(top, (hl, LANES))
            mtop[p] = top
            ltot[p] = jnp.broadcast_to(jnp.sum(wt, axis=1, keepdims=True), (hl, LANES))
            mrun[p + 1] = jnp.maximum(mrun[before], top)
        return carry

    lax.fori_loop(0, steps, score_step, 0)

    def value_step(c, carry):
        kv_copy(v_hbm, v_v, v_sem, c).wait()
        for i in range(PAGES_PER_STEP):
            p = c * PAGES_PER_STEP + i
            code = meta_s[0, p]
            own = jnp.bitwise_and(lax.shift_right_logical(code, 8), 31)
            before = jnp.clip(lax.shift_right_logical(code, 13), 0, pages)
            final = jnp.clip(meta_s[1, own], 0, pages)
            o = jnp.dot(wt_v[p], v_v[page_part(p), :], preferred_element_type=F32)
            fb = jnp.exp2((mtop[p] - mrun[final]) * scale)
            lrun[p + 1] = lrun[before] + fb * ltot[p]
            orun[p + 1] = orun[before] + fb * o
        return carry

    lax.fori_loop(0, steps, value_step, 0)

    lane_h = lax.broadcasted_iota(I32, (hl, LANES), 1)
    mpack = jnp.zeros((hl, LANES), F32)
    lpack = jnp.zeros((hl, LANES), F32)
    for s in range(ns):
        f = jnp.clip(meta_s[1, s], 0, pages)
        ofin[s] = orun[f]
        mpack = jnp.where(lane_h == s, mrun[f], mpack)
        lpack = jnp.where(lane_h == s, lrun[f], lpack)
    both = jnp.concatenate([mpack, lpack, jnp.zeros((LANES - 2 * hl, LANES), F32)], axis=0)
    mlt = jnp.transpose(both)[0:ns, :]
    for ct in range(cores):
        part = mlt[ct * sb : (ct + 1) * sb, :]
        for cx in range(nx):
            s1m[ct, cx] = part if cx == 0 else pltpu.roll(part, LANES - cx * hq, 1)
            for j in range(hq):
                s1o[ct, cx, j] = ofin[ct * sb : (ct + 1) * sb, cx * hq + j, :].astype(BF16)
    r1o[t, x] = s1o[t, x]
    r1m[t, x] = s1m[t, x]

    pl.semaphore_wait(barrier, len(xpeers) + jnp.where(is_spot, nz - 1 + nx - 1, cores))

    def s1_copies(i, px, pt, ft, fx):
        to = at(px, z, pt)
        return (
            remote(s1m.at[pt, px], r1m.at[ft, fx], s1ms_sem.at[i], s1mr_sem.at[ft, fx], to),
            remote(s1o.at[pt, px], r1o.at[ft, fx], s1s_sem.at[i], s1r_sem.at[ft, fx], to))

    for i, (px, pt) in enumerate(xpeers):
        for copy in s1_copies(i, px, pt, t, x):
            copy.start()

    w_copy.wait()
    w_send = remote(w_v.at[t], w_v.at[t], ws_sem, wr_sem, at(x, z, (t + 1) % cores))
    w_recv = remote(w_v.at[t], w_v.at[(t + 1) % cores], ws_sem, wr_sem, at(x, z, (t + 1) % cores))
    w_send.start()

    for i, (px, pt) in enumerate(xpeers):
        for copy in s1_copies(i, px, pt, pt, px):
            copy.wait_recv()

    lane_s = lax.broadcasted_iota(I32, (sb, LANES), 1)

    def merged(ml):
        top = functools.reduce(jnp.maximum, ml)
        fs = [jnp.exp2((m - top) * scale) for m in ml]
        tot = functools.reduce(jnp.add, [f * pltpu.roll(m, LANES - hl, 1) for f, m in zip(fs, ml)])
        return top, fs, tot

    def s2_copies(o, slot):
        to = at(x, spots[o], t)
        return (
            remote(s2m.at[o], r2m.at[slot], s2ms_sem.at[o], s2mr_sem.at[slot], to),
            remote(s2o.at[o], r2o.at[slot], s2s_sem.at[o], s2r_sem.at[slot], to))

    for o in reversed(range(cores)):
        top, fs, tot = merged([r1m[o, cx] for cx in range(nx)])
        s2m[o] = jnp.where(lane_s < hq, top, pltpu.roll(tot, hl, 1))
        for j in range(hq):
            num = functools.reduce(
                jnp.add,
                [jnp.broadcast_to(fs[cx][:, j : j + 1], (sb, hd)) * r1o[o, cx, j].astype(F32) for cx in range(nx)])
            s2o[o, j] = num.astype(BF16)

        @pl.when(z != spots[o])
        def _():
            for copy in s2_copies(o, z):
                copy.start()

        @pl.when(z == spots[o])
        def _():
            r2m[z] = s2m[o]
            r2o[z] = s2o[o]

    def direct(dx):
        return remote(
            g_v.at[x, 0], g_v.at[x, 0], gd_sem.at[dx], gr_sem.at[x, 0], at((x + dx) % nx, spots[1], t))

    def along_z(o, pz):
        return remote(g_v.at[x, o], g_v.at[x, o], gz_sem.at[pz], gr_sem.at[x, o], at(x, pz, t))

    def along_x(o, dx):
        return remote(
            g_v.at[x, o], g_v.at[x, o], gx_sem.at[o, dx], gr_sem.at[x, o], at((x + dx) % nx, z, t))

    def arrival(o, sx):
        return remote(g_v.at[sx, o], g_v.at[sx, o], gd_sem.at[0], gr_sem.at[sx, o], at(x, z, (t + 1) % cores))

    xorder = [d for d in range(nx) if d]
    for o in reversed(range(cores)):
        zorder = [(spots[o] + d) % nz for d in range(1, nz)]
        if o == 0:
            zorder = [pz for pz in zorder if pz != spots[1]]

        @pl.when(z == spots[o])
        def _():
            for pz in range(nz):
                if pz != spots[o]:
                    for copy in (
                        remote(s2m.at[o], r2m.at[pz], s2ms_sem.at[o], s2mr_sem.at[pz], at(x, pz, t)),
                        remote(s2o.at[o], r2o.at[pz], s2s_sem.at[o], s2r_sem.at[pz], at(x, pz, t))):
                        copy.wait_recv()
            top, fs, tot = merged([r2m[i] for i in range(nz)])
            inv = jnp.where(lane_s < hq, 1.0 / tot, 0.0)
            fs = [f * inv for f in fs]
            for j in range(hq):
                att = functools.reduce(
                    jnp.add,
                    [jnp.broadcast_to(fs[i][:, j : j + 1], (sb, hd)) * r2o[i, j].astype(F32) for i in range(nz)])
                g_v[x, o, j] = att.astype(BF16)
            if o == 0:
                for dx in xorder + [0]:
                    direct(dx).start()
            else:
                for dx in xorder:
                    along_x(o, dx).start()
            for pz in zorder:
                along_z(o, pz).start()
            if o == 0:
                for dx in xorder:
                    along_x(o, dx).start()

    for o in reversed(range(cores)):
        @pl.when((z != spots[o]) & ((z != spots[1]) | (o == 1)))
        def _():
            arrival(o, x).wait_recv()
            for dx in xorder:
                along_x(o, dx).start()

    @pl.when(z == spots[1])
    def _():
        arrival(0, x).wait_recv()

    w_recv.wait_recv()

    out = jnp.zeros((sb, hd), F32)
    for dx in [0] + xorder:
        sx = (x + dx) % nx
        for o in reversed(range(cores)):
            if dx:
                arrival(o, sx).wait_recv()
            for j in range(0, hq, 2):
                lhs = jnp.concatenate([g_v[sx, o, j], g_v[sx, o, j + 1]], axis=1)
                first = pl.multiple_of((sx * hq + j) * hd, 2 * hd)
                out = out + jnp.dot(lhs, w_v[o, pl.ds(first, 2 * hd), :], preferred_element_type=F32)
    out_ref[...] = out.astype(out_ref.dtype)

    w_send.wait_send()
    for i, (px, pt) in enumerate(xpeers):
        for copy in s1_copies(i, px, pt, t, x):
            copy.wait_send()
    for o in range(cores):
        @pl.when(z != spots[o])
        def _():
            for copy in s2_copies(o, z):
                copy.wait_send()

        @pl.when(z == spots[o])
        def _():
            for pz in range(nz):
                if pz != spots[o] and not (o == 0 and pz == spots[1]):
                    along_z(o, pz).wait_send()
            if o == 0:
                for dx in range(nx):
                    direct(dx).wait_send()

        @pl.when((z != spots[1]) | (o == 1))
        def _():
            for dx in xorder:
                along_x(o, dx).wait_send()


def body(query, key_cache, value_cache, lengths, page_order, out_weight):
    pages, page_len, kvh, hd = key_cache.shape
    ns, hl = query.shape[0], query.shape[1]
    cores = lax.axis_size("tensor")
    nz = ns
    nx = lax.axis_size("seq") // nz
    hq = hl // nx
    sb = ns // cores
    rows = page_len * kvh
    pr = page_order.shape[0] // LANES
    wr, wc = out_weight.shape
    dims = (nx, nz, pages, page_len, kvh, ns, hl, hd, cores)
    steps = pages // PAGES_PER_STEP
    nxp = nx * cores - 1
    dma = pltpu.SemaphoreType.DMA
    return pl.pallas_call(
        functools.partial(kernel, dims),
        out_shape=jax.ShapeDtypeStruct((sb, wc), BF16),
        in_specs=[pl.BlockSpec(memory_space=pltpu.SMEM)] + [pl.BlockSpec(memory_space=pl.ANY)] * 5,
        out_specs=pl.BlockSpec(memory_space=pltpu.VMEM),
        scratch_shapes=[
            pltpu.VMEM((ns, hl, hd), BF16),
            pltpu.VMEM((pages * rows, hd), BF16),
            pltpu.VMEM((pages * rows, hd), BF16),
            pltpu.VMEM((pr, LANES), I32),
            pltpu.VMEM((cores, wr, wc), BF16),
            pltpu.VMEM((pr, LANES), F32),
            pltpu.VMEM((8, LANES), I32),
            pltpu.SMEM((8, LANES), I32),
            pltpu.VMEM((hl, rows), I32),
            pltpu.VMEM((pages, hl, rows), BF16),
            pltpu.VMEM((pages, hl, LANES), F32),
            pltpu.VMEM((pages, hl, LANES), F32),
            pltpu.VMEM((pages + 1, hl, LANES), F32),
            pltpu.VMEM((pages + 1, hl, LANES), F32),
            pltpu.VMEM((pages + 1, hl, hd), F32),
            pltpu.VMEM((ns, hl, hd), F32),
            pltpu.VMEM((cores, nx, hq, sb, hd), BF16),
            pltpu.VMEM((cores, nx, sb, LANES), F32),
            pltpu.VMEM((cores, nx, hq, sb, hd), BF16),
            pltpu.VMEM((cores, nx, sb, LANES), F32),
            pltpu.VMEM((cores, hq, sb, hd), BF16),
            pltpu.VMEM((cores, sb, LANES), F32),
            pltpu.VMEM((nz, hq, sb, hd), BF16),
            pltpu.VMEM((nz, sb, LANES), F32),
            pltpu.VMEM((nx, cores, hq, sb, hd), BF16),
            dma, dma((steps,)), dma((steps,)), dma, dma, dma,
            dma, dma, dma((nxp,)), dma((cores, nx)), dma((nxp,)), dma((cores, nx)),
            dma((cores,)), dma((nz,)), dma((cores,)), dma((nz,)),
            dma((nx,)), dma((nz,)), dma((cores, nx)), dma((nx, cores)),
        ],
        compiler_params=pltpu.CompilerParams(collective_id=0, has_side_effects=True),
        name="paged_decode",
    )(
        lengths, query, key_cache.reshape(pages * rows, hd), value_cache.reshape(pages * rows, hd),
        page_order.reshape(pr, LANES), out_weight)


def solution(mesh):
    in_specs = (
        P("group", "tensor", None),
        P(("group", "seq"), None, "tensor", None),
        P(("group", "seq"), None, "tensor", None),
        P("group"),
        P("group"),
        P("tensor", "seq"),
    )
    out_specs = P(("group", "tensor"), "seq")
    return jax.shard_map(body, mesh=mesh, in_specs=in_specs, out_specs=out_specs, check_vma=False)
```

time: 61.2 us -> 52 us (0.85)
  the two profiles are of different devices: /device:TPU:40 before, /device:TPU:168 now
where the time goes in v2:
time: 52 us; the launch traced here: 51.9 us
  Pallas kernels  50.6 us (97%)
  local copies, waits for them, and re-layouts  1.26 us (2%)
    pallas_call x1, Pallas kernels, body(): pl.pallas_call(functools.partial(kernel, dims), out_shape=jax.ShapeDtypeS...  50.6 us
    unnamed x1, local copies, waits for them, and re-layouts  1.26 us

profile of v2, /device:TPU:168, one launch (start us, length us, event | category | flops | bytes accessed | tf_op | source)
XLA Modules:
  0.0 51.9 jit_solution(6333679636346182280)
XLA Ops:
  0.0 50.6 %paged_decode.1 = bf16[8,128]{1,0:T(8,128)(2,1)} custom-call(s32[16]{0:T(128)} %len_s.1, bf16[16,32,128]{2,1,0:T(8,128)(2,1)} %q_hbm.1, bf16[16384,128]{1,0:T(8,128)(2,1)} %bitcast.3, bf16[16384,128]{1,0:T(8,128)(2,1)} %bitcast.4, s32[16,128]{1,0:T(8,128)} %bitcast.5, bf16[4096,128]{1,0:T(8,128)(2,1)} %w_hbm.1), custom_call_target="tpu_custom_call" | custom-call | tf_op jit(solution)/shard_map/paged_decode/pallas_call | solution.py:369
  50.6 1.3 %copy.8 = bf16[8,128]{1,0:T(8,128)(2,1)} copy(bf16[8,128]{1,0:T(8,128)(2,1)} %paged_decode.1) | data formatting | bytes 4096

commit v3 on v2

v3 whole, which is shorter than its diff:
```python
import functools
import math

import jax
import jax.numpy as jnp
from jax import lax
from jax.experimental import pallas as pl
from jax.experimental.pallas import tpu as pltpu
from jax.sharding import PartitionSpec as P

MESH = pl.DeviceIdType.MESH
F32 = jnp.float32
BF16 = jnp.bfloat16
I32 = jnp.int32
LANES = 128
NEG = -1e30
PAGES_PER_STEP = 8


def kernel(
    dims,
    len_hbm, q_hbm, k_hbm, v_hbm, po_hbm, w_hbm, out_ref,
    len_s, q_v, k_v, v_v, po_v, w_v, val_v, meta_v, meta_s, cmod_v,
    wt_v, mtop, ltot, mrun, lrun, orun, ofin, s1, r1, s2, r2, s1m, r1m, s2m, r2m, g_v,
    len_sem, q_sem, k_sem, v_sem, po_sem, w_sem, meta_sem, ws_sem, wr_sem,
    s1s_sem, s1r_sem, s2s_sem, s2r_sem, m1s_sem, m1r_sem, m2s_sem, m2r_sem, gzs_sem, gxs_sem, own_sem, peer_sem,
):
    nx, nz, pages, page_len, kvh, ns, hl, hd, cores = dims
    rows = page_len * kvh
    hq = hl // nx
    sb = ns // cores
    group_size = hl // kvh
    scale = math.log2(math.e) / math.sqrt(hd)
    me = lax.axis_index("seq")
    t = lax.axis_index("tensor")
    x = me // nz
    z = me % nz
    steps = pages // PAGES_PER_STEP
    spots = (1, 0)

    def at(px, pz, pt):
        return {"seq": px * nz + pz, "tensor": pt}

    def remote(src, dst, send, recv, to):
        return pltpu.make_async_remote_copy(
            src_ref=src, dst_ref=dst, send_sem=send, recv_sem=recv, device_id=to, device_id_type=MESH)

    len_copy = pltpu.make_async_copy(len_hbm, len_s, len_sem)
    len_copy.start()
    po_copy = pltpu.make_async_copy(po_hbm, po_v, po_sem)
    po_copy.start()
    q_copy = pltpu.make_async_copy(q_hbm, q_v, q_sem)
    q_copy.start()

    xpeers = []
    for dx in range(nx):
        for dt in range(cores):
            if dx or dt:
                xpeers.append(((x + dx) % nx, (t + dt) % cores))
    barrier = pltpu.get_barrier_semaphore()

    def greet(px, pz, pt):
        pl.semaphore_signal(barrier, inc=1, device_id=at(px, pz, pt), device_id_type=MESH)

    for px, pt in xpeers:
        greet(px, z, pt)

    step_rows = PAGES_PER_STEP * rows

    def kv_copy(src, dst, sem, c):
        part = pl.ds(c * step_rows, step_rows)
        return pltpu.make_async_copy(src.at[part], dst.at[part], sem.at[c])

    for c in range(steps):
        kv_copy(k_hbm, k_v, k_sem, c).start()
    for c in range(steps):
        kv_copy(v_hbm, v_v, v_sem, c).start()
    w_copy = pltpu.make_async_copy(w_hbm, w_v.at[t], w_sem)
    w_copy.start()

    for o in range(cores):
        @pl.when(z == spots[o])
        def _():
            for d in range(1, nz):
                greet(x, (z + d) % nz, t)
            if o == 1:
                for dx in range(1, nx):
                    greet((x + dx) % nx, spots[0], t)

    cl = lax.broadcasted_iota(I32, (hl, rows), 1)
    hr = lax.broadcasted_iota(I32, (hl, rows), 0)
    cmod_v[...] = jnp.where(cl % kvh == hr // group_size, cl, 1 << 20)
    mrun[0] = jnp.full((hl, LANES), NEG, F32)
    lrun[0] = jnp.zeros((hl, LANES), F32)
    orun[0] = jnp.zeros((hl, hd), F32)

    len_copy.wait()
    lens = [len_s[s] for s in range(ns)]
    starts = []
    run = jnp.int32(0)
    for s in range(ns):
        starts.append(run)
        run = run + lax.shift_right_logical(lens[s] + (page_len - 1), int(math.log2(page_len)))
    pr = po_v.shape[0]
    rank = lax.broadcasted_iota(I32, (pr, LANES), 0) * LANES + lax.broadcasted_iota(I32, (pr, LANES), 1)
    owner = jnp.zeros((pr, LANES), I32)
    end = jnp.full((pr, LANES), lens[0], I32)
    for s in range(1, ns):
        past = rank >= starts[s]
        owner = jnp.where(past, s, owner)
        end = jnp.where(past, lens[s] + starts[s] * page_len, end)
    valid = jnp.clip(end - rank * page_len, 0, page_len)
    owner = jnp.where(valid > 0, owner, ns)
    val_v[...] = (owner * 256 + valid).astype(F32)

    po_copy.wait()
    ids = lax.broadcasted_iota(I32, (pages, LANES), 0) + me * pages
    acc = jnp.zeros((pages, LANES), F32)
    for i in range(pr):
        hit = jnp.broadcast_to(po_v[i : i + 1, :], (pages, LANES)) == ids
        acc = acc + jnp.where(hit, jnp.broadcast_to(val_v[i : i + 1, :], (pages, LANES)), 0.0)
    val_col = jnp.broadcast_to(jnp.sum(acc, axis=1, keepdims=True), (pages, LANES))
    pad = jnp.concatenate([val_col, jnp.zeros((LANES - pages, LANES), F32)], axis=0)
    val_row = jnp.transpose(pad)[0:1, :]
    own_col = lax.shift_right_logical(val_col.astype(I32), 8)
    val_row_i = val_row.astype(I32)
    own_row = lax.shift_right_logical(val_row_i, 8)
    prow = lax.broadcasted_iota(I32, (pages, LANES), 0)
    lane = lax.broadcasted_iota(I32, (pages, LANES), 1)
    same = (own_col == jnp.broadcast_to(own_row, (pages, LANES))) & (prow < lane)
    prev = jnp.max(jnp.where(same, (prow + 1).astype(F32), 0.0), axis=0, keepdims=True).astype(I32)
    last = jnp.max(jnp.where(own_col == lane, (prow + 1).astype(F32), 0.0), axis=0, keepdims=True).astype(I32)
    meta_v[0:1, :] = prev * 8192 + val_row_i
    meta_v[1:2, :] = last
    meta_copy = pltpu.make_async_copy(meta_v, meta_s, meta_sem)
    meta_copy.start()
    meta_copy.wait()
    q_copy.wait()

    def page_part(p):
        return pl.ds(pl.multiple_of(p * rows, rows), rows)

    def score_step(c, carry):
        kv_copy(k_hbm, k_v, k_sem, c).wait()
        for i in range(PAGES_PER_STEP):
            p = c * PAGES_PER_STEP + i
            code = meta_s[0, p]
            nvalid = jnp.bitwise_and(code, 255) * kvh
            own = jnp.minimum(jnp.bitwise_and(lax.shift_right_logical(code, 8), 31), ns - 1)
            before = jnp.clip(lax.shift_right_logical(code, 13), 0, pages)
            sc = lax.dot_general(
                q_v[own], k_v[page_part(p), :], (((1,), (1,)), ((), ())), preferred_element_type=F32)
            sc = jnp.where(cmod_v[...] < nvalid, sc, NEG)
            top = jnp.max(sc, axis=1, keepdims=True)
            wt = jnp.exp2((sc - top) * scale)
            wt_v[p] = wt.astype(BF16)
            top = jnp.broadcast_to(top, (hl, LANES))
            mtop[p] = top
            ltot[p] = jnp.broadcast_to(jnp.sum(wt, axis=1, keepdims=True), (hl, LANES))
            mrun[p + 1] = jnp.maximum(mrun[before], top)
        return carry

    lax.fori_loop(0, steps, score_step, 0)

    def value_step(c, carry):
        kv_copy(v_hbm, v_v, v_sem, c).wait()
        for i in range(PAGES_PER_STEP):
            p = c * PAGES_PER_STEP + i
            code = meta_s[0, p]
            own = jnp.bitwise_and(lax.shift_right_logical(code, 8), 31)
            before = jnp.clip(lax.shift_right_logical(code, 13), 0, pages)
            final = jnp.clip(meta_s[1, own], 0, pages)
            o = jnp.dot(wt_v[p], v_v[page_part(p), :], preferred_element_type=F32)
            fb = jnp.exp2((mtop[p] - mrun[final]) * scale)
            lrun[p + 1] = lrun[before] + fb * ltot[p]
            orun[p + 1] = orun[before] + fb * o
        return carry

    lax.fori_loop(0, steps, value_step, 0)

    lane_h = lax.broadcasted_iota(I32, (hl, LANES), 1)
    mpack = jnp.zeros((hl, LANES), F32)
    lpack = jnp.zeros((hl, LANES), F32)
    for s in range(ns):
        f = jnp.clip(meta_s[1, s], 0, pages)
        ofin[s] = orun[f]
        mpack = jnp.where(lane_h == s, mrun[f], mpack)
        lpack = jnp.where(lane_h == s, lrun[f], lpack)
    gap = jnp.zeros((LANES // 2 - hl, LANES), F32)
    mlt = jnp.transpose(jnp.concatenate([mpack, gap, lpack, gap], axis=0))[0:ns, :]
    lane_s = lax.broadcasted_iota(I32, (sb, LANES), 1)
    half = LANES // 2
    for ct in range(cores):
        part = mlt[ct * sb : (ct + 1) * sb, :]
        for cx in range(nx):
            s1m[ct * nx + cx] = part if cx == 0 else pltpu.roll(part, LANES - cx * hq, 1)
            for j in range(hq):
                s1[ct * nx + cx, j] = ofin[ct * sb : (ct + 1) * sb, cx * hq + j, :].astype(BF16)
    r1[t * nx + x] = s1[t * nx + x]
    r1m[t * nx + x] = s1m[t * nx + x]

    pl.semaphore_wait(barrier, len(xpeers) + jnp.where(z == spots[0], nx, jnp.where(z == spots[1], 1, cores)))

    for px, pt in xpeers:
        remote(s1.at[pt * nx + px], r1.at[t * nx + x], s1s_sem, s1r_sem, at(px, z, pt)).start()
        remote(s1m.at[pt * nx + px], r1m.at[t * nx + x], m1s_sem, m1r_sem, at(px, z, pt)).start()

    def bulk(ref, blocks, send, recv):
        part = ref.at[pl.ds(0, blocks)]
        return remote(part, part, send, recv, at(x, z, (t + 1) % cores))

    bulk(r1m, len(xpeers), m1s_sem, m1r_sem).wait_recv()
    bulk(r1, len(xpeers), s1s_sem, s1r_sem).wait_recv()

    def merged(ml):
        top = functools.reduce(jnp.maximum, ml)
        fs = [jnp.exp2((m - top) * scale) for m in ml]
        tot = functools.reduce(jnp.add, [f * pltpu.roll(m, half, 1) for f, m in zip(fs, ml)])
        return top, fs, tot

    for o in reversed(range(cores)):
        top, fs, tot = merged([r1m[o * nx + cx] for cx in range(nx)])
        s2m[o] = jnp.where(lane_s < half, top, pltpu.roll(tot, half, 1))
        for j in range(hq):
            num = functools.reduce(
                jnp.add,
                [jnp.broadcast_to(fs[cx][:, j : j + 1], (sb, hd)) * r1[o * nx + cx, j].astype(F32) for cx in range(nx)])
            s2[o, j] = num.astype(BF16)

        @pl.when(z != spots[o])
        def _():
            remote(s2m.at[o], r2m.at[z], m2s_sem, m2r_sem, at(x, spots[o], t)).start()
            remote(s2.at[o], r2.at[z], s2s_sem, s2r_sem, at(x, spots[o], t)).start()

        @pl.when(z == spots[o])
        def _():
            r2[z] = s2[o]
            r2m[z] = s2m[o]

    w_send = remote(w_v.at[t], w_v.at[t], ws_sem, wr_sem, at(x, z, (t + 1) % cores))
    w_recv = remote(w_v.at[t], w_v.at[(t + 1) % cores], ws_sem, wr_sem, at(x, z, (t + 1) % cores))
    w_copy.wait()
    w_send.start()

    def direct(dx):
        to = at((x + dx) % nx, spots[1], t)
        return remote(g_v.at[x, 0], g_v.at[x, 0], gzs_sem, peer_sem.at[0] if dx else own_sem.at[0], to)

    def along_z(o, pz):
        return remote(g_v.at[x, o], g_v.at[x, o], gzs_sem, own_sem.at[o], at(x, pz, t))

    def along_x(o, dx):
        return remote(g_v.at[x, o], g_v.at[x, o], gxs_sem, peer_sem.at[o], at((x + dx) % nx, z, t))

    def own_arrival(o):
        return remote(g_v.at[x, o], g_v.at[x, o], gzs_sem, own_sem.at[o], at(x, z, (t + 1) % cores))

    xorder = [d for d in range(nx) if d]
    for o in reversed(range(cores)):
        zorder = [(spots[o] + d) % nz for d in range(1, nz)]
        if o == 0:
            zorder = [pz for pz in zorder if pz != spots[1]]

        @pl.when(z == spots[o])
        def _():
            bulk(r2m, nz - 1, m2s_sem, m2r_sem).wait_recv()
            bulk(r2, nz - 1, s2s_sem, s2r_sem).wait_recv()
            top, fs, tot = merged([r2m[i] for i in range(nz)])
            inv = jnp.where(lane_s < hq, 1.0 / tot, 0.0)
            fs = [f * inv for f in fs]
            for j in range(hq):
                att = functools.reduce(
                    jnp.add,
                    [jnp.broadcast_to(fs[i][:, j : j + 1], (sb, hd)) * r2[i, j].astype(F32) for i in range(nz)])
                g_v[x, o, j] = att.astype(BF16)
            if o == 0:
                for dx in xorder + [0]:
                    direct(dx).start()
            else:
                for dx in xorder:
                    along_x(o, dx).start()
            for pz in zorder:
                along_z(o, pz).start()
            if o == 0:
                for dx in xorder:
                    along_x(o, dx).start()

    for o in reversed(range(cores)):
        @pl.when((z != spots[o]) & ((z != spots[1]) | (o == 1)))
        def _():
            own_arrival(o).wait_recv()
            for dx in xorder:
                along_x(o, dx).start()

    @pl.when(z == spots[1])
    def _():
        own_arrival(0).wait_recv()

    w_recv.wait_recv()

    def bytes_of(blocks, send, recv):
        part = k_v.at[pl.ds(0, blocks * hq * sb)]
        return remote(part, part, send, recv, at(x, z, (t + 1) % cores))

    out = jnp.zeros((sb, hd), F32)
    for mine in (True, False):
        for o in reversed(range(cores)):
            if not mine:
                bytes_of(nx - 1, gxs_sem, peer_sem.at[o]).wait_recv()
            for dx in [0] if mine else xorder:
                sx = (x + dx) % nx
                for j in range(0, hq, 2):
                    lhs = jnp.concatenate([g_v[sx, o, j], g_v[sx, o, j + 1]], axis=1)
                    first = pl.multiple_of((sx * hq + j) * hd, 2 * hd)
                    out = out + jnp.dot(lhs, w_v[o, pl.ds(first, 2 * hd), :], preferred_element_type=F32)
    out_ref[...] = out.astype(out_ref.dtype)

    w_send.wait_send()
    bulk(s1, len(xpeers), s1s_sem, s1r_sem).wait_send()
    bulk(s1m, len(xpeers), m1s_sem, m1r_sem).wait_send()

    @pl.when((z != spots[0]) & (z != spots[1]))
    def _():
        bulk(s2, cores, s2s_sem, s2r_sem).wait_send()
        bulk(s2m, cores, m2s_sem, m2r_sem).wait_send()

    @pl.when((z == spots[0]) | (z == spots[1]))
    def _():
        bulk(s2, 1, s2s_sem, s2r_sem).wait_send()
        bulk(s2m, 1, m2s_sem, m2r_sem).wait_send()

    @pl.when(z == spots[0])
    def _():
        bytes_of(nz - 2 + nx, gzs_sem, own_sem.at[0]).wait_send()

    @pl.when(z == spots[1])
    def _():
        bytes_of(nz - 1, gzs_sem, own_sem.at[0]).wait_send()
        bytes_of(nx - 1, gxs_sem, peer_sem.at[1]).wait_send()

    @pl.when(z != spots[1])
    def _():
        bytes_of(cores * (nx - 1), gxs_sem, peer_sem.at[0]).wait_send()


def body(query, key_cache, value_cache, lengths, page_order, out_weight):
    pages, page_len, kvh, hd = key_cache.shape
    ns, hl = query.shape[0], query.shape[1]
    cores = lax.axis_size("tensor")
    nz = ns
    nx = lax.axis_size("seq") // nz
    hq = hl // nx
    sb = ns // cores
    rows = page_len * kvh
    pr = page_order.shape[0] // LANES
    wr, wc = out_weight.shape
    dims = (nx, nz, pages, page_len, kvh, ns, hl, hd, cores)
    steps = pages // PAGES_PER_STEP
    dma = pltpu.SemaphoreType.DMA
    return pl.pallas_call(
        functools.partial(kernel, dims),
        out_shape=pltpu.VMEM((sb, wc), BF16),
        in_specs=[pl.BlockSpec(memory_space=pl.ANY)] * 6,
        out_specs=pl.BlockSpec(memory_space=pltpu.VMEM),
        scratch_shapes=[
            pltpu.SMEM((ns,), I32),
            pltpu.VMEM((ns, hl, hd), BF16),
            pltpu.VMEM((pages * rows, hd), BF16),
            pltpu.VMEM((pages * rows, hd), BF16),
            pltpu.VMEM((pr, LANES), I32),
            pltpu.VMEM((cores, wr, wc), BF16),
            pltpu.VMEM((pr, LANES), F32),
            pltpu.VMEM((8, LANES), I32),
            pltpu.SMEM((8, LANES), I32),
            pltpu.VMEM((hl, rows), I32),
            pltpu.VMEM((pages, hl, rows), BF16),
            pltpu.VMEM((pages, hl, LANES), F32),
            pltpu.VMEM((pages, hl, LANES), F32),
            pltpu.VMEM((pages + 1, hl, LANES), F32),
            pltpu.VMEM((pages + 1, hl, LANES), F32),
            pltpu.VMEM((pages + 1, hl, hd), F32),
            pltpu.VMEM((ns, hl, hd), F32),
            pltpu.VMEM((cores * nx, hq, sb, hd), BF16),
            pltpu.VMEM((cores * nx, hq, sb, hd), BF16),
            pltpu.VMEM((cores, hq, sb, hd), BF16),
            pltpu.VMEM((nz, hq, sb, hd), BF16),
            pltpu.VMEM((cores * nx, sb, LANES), F32),
            pltpu.VMEM((cores * nx, sb, LANES), F32),
            pltpu.VMEM((cores, sb, LANES), F32),
            pltpu.VMEM((nz, sb, LANES), F32),
            pltpu.VMEM((nx, cores, hq, sb, hd), BF16),
            dma, dma, dma((steps,)), dma((steps,)), dma, dma, dma, dma, dma,
            dma, dma, dma, dma, dma, dma, dma, dma, dma, dma, dma((cores,)), dma((cores,)),
        ],
        compiler_params=pltpu.CompilerParams(collective_id=0, has_side_effects=True),
        name="paged_decode",
    )(
        lengths, query, key_cache.reshape(pages * rows, hd), value_cache.reshape(pages * rows, hd),
        page_order.reshape(pr, LANES), out_weight)


def solution(mesh):
    in_specs = (
        P("group", "tensor", None),
        P(("group", "seq"), None, "tensor", None),
        P(("group", "seq"), None, "tensor", None),
        P("group"),
        P("group"),
        P("tensor", "seq"),
    )
    out_specs = P(("group", "tensor"), "seq")
    return jax.shard_map(body, mesh=mesh, in_specs=in_specs, out_specs=out_specs, check_vma=False)
```

time: 52 us -> 46 us (0.88)
  the two profiles are of different devices: /device:TPU:168 before, /device:TPU:40 now
where the time goes in v3:
time: 46 us; the launch traced here: 45.6 us
  Pallas kernels  45 us (98%)
  local copies, waits for them, and re-layouts  0.58 us (1%)
    pallas_call x1, Pallas kernels, body(): pl.pallas_call(functools.partial(kernel, dims), out_shape=pltpu.VMEM((sb,...  45 us

profile of v3, /device:TPU:40, one launch (start us, length us, event | category | flops | bytes accessed | tf_op | source)
XLA Modules:
  0.0 45.6 jit_solution(8672488770651458751)
XLA Ops:
  0.0 45.0 %paged_decode.1 = bf16[8,128]{1,0:T(8,128)(2,1)S(1)} custom-call(s32[16]{0:T(128)} %len_hbm.1, bf16[16,32,128]{2,1,0:T(8,128)(2,1)} %q_hbm.1, bf16[16384,128]{1,0:T(8,128)(2,1)} %bitcast.3, bf16[16384,128]{1,0:T(8,128)(2,1)} %bitcast.4, s32[16,128]{1,0:T(8,128)} %bitcast.5, bf16[4096,128]{1,0:T(8,128)(2,1)} %w_hbm.1), custom_call_target="tpu_custom_call" | custom-call | tf_op jit(solution)/shard_map/paged_decode/pallas_call | solution.py:360
  45.0 0.6 %copy.8 = bf16[8,128]{1,0:T(8,128)(2,1)} copy(bf16[8,128]{1,0:T(8,128)(2,1)S(1)} %paged_decode.1) | data formatting | bytes 4096

commit v4 on v3

--- a/solution.py
+++ b/solution.py
@@ -21,9 +21,9 @@
     dims,
     len_hbm, q_hbm, k_hbm, v_hbm, po_hbm, w_hbm, out_ref,
     len_s, q_v, k_v, v_v, po_v, w_v, val_v, meta_v, meta_s, cmod_v,
-    wt_v, mtop, ltot, mrun, lrun, orun, ofin, s1, r1, s2, r2, s1m, r1m, s2m, r2m, g_v,
+    wt_v, mtop, ltot, mrun, lrun, orun, ofin, s1, r1, s2, r2, s2m, r2m, g_v,
     len_sem, q_sem, k_sem, v_sem, po_sem, w_sem, meta_sem, ws_sem, wr_sem,
-    s1s_sem, s1r_sem, s2s_sem, s2r_sem, m1s_sem, m1r_sem, m2s_sem, m2r_sem, gzs_sem, gxs_sem, own_sem, peer_sem,
+    s1s_sem, s1r_sem, s2s_sem, s2r_sem, m2s_sem, m2r_sem, gzs_sem, gxs_sem, own_sem, peer_sem,
 ):
     nx, nz, pages, page_len, kvh, ns, hl, hd, cores = dims
     rows = page_len * kvh
@@ -37,6 +37,8 @@
     z = me % nz
     steps = pages // PAGES_PER_STEP
     spots = (1, 0)
+    zp = z % 2
+    hh = hq // 2
 
     def at(px, pz, pt):
         return {"seq": px * nz + pz, "tensor": pt}
@@ -52,18 +54,20 @@
     q_copy = pltpu.make_async_copy(q_hbm, q_v, q_sem)
     q_copy.start()
 
-    xpeers = []
-    for dx in range(nx):
-        for dt in range(cores):
-            if dx or dt:
-                xpeers.append(((x + dx) % nx, (t + dt) % cores))
+    peers = []
+    for dx in [nx // 2] + [d for d in range(nx) if d != nx // 2]:
+        for dp in range(2):
+            for dt in range(cores):
+                if dx or dp or dt:
+                    peers.append(((x + dx) % nx, (zp + dp) % 2, (t + dt) % cores))
     barrier = pltpu.get_barrier_semaphore()
 
     def greet(px, pz, pt):
         pl.semaphore_signal(barrier, inc=1, device_id=at(px, pz, pt), device_id_type=MESH)
 
-    for px, pt in xpeers:
-        greet(px, z, pt)
+    early_greets = 4
+    for px, pp, pt in peers[:early_greets]:
+        greet(px, z - zp + pp, pt)
 
     step_rows = PAGES_PER_STEP * rows
 
@@ -78,14 +82,13 @@
     w_copy = pltpu.make_async_copy(w_hbm, w_v.at[t], w_sem)
     w_copy.start()
 
-    for o in range(cores):
-        @pl.when(z == spots[o])
-        def _():
-            for d in range(1, nz):
-                greet(x, (z + d) % nz, t)
-            if o == 1:
-                for dx in range(1, nx):
-                    greet((x + dx) % nx, spots[0], t)
+    for px, pp, pt in peers[early_greets:]:
+        greet(px, z - zp + pp, pt)
+
+    @pl.when(z < 2)
+    def _():
+        for d in range(2, nz, 2):
+            greet(x, z + d, t)
 
     cl = lax.broadcasted_iota(I32, (hl, rows), 1)
     hr = lax.broadcasted_iota(I32, (hl, rows), 0)
@@ -179,38 +182,45 @@
     lax.fori_loop(0, steps, value_step, 0)
 
     lane_h = lax.broadcasted_iota(I32, (hl, LANES), 1)
-    mpack = jnp.zeros((hl, LANES), F32)
-    lpack = jnp.zeros((hl, LANES), F32)
+    half = LANES // 2
+    ml = jnp.zeros((hl, LANES), F32)
     for s in range(ns):
         f = jnp.clip(meta_s[1, s], 0, pages)
         ofin[s] = orun[f]
-        mpack = jnp.where(lane_h == s, mrun[f], mpack)
-        lpack = jnp.where(lane_h == s, lrun[f], lpack)
-    gap = jnp.zeros((LANES // 2 - hl, LANES), F32)
-    mlt = jnp.transpose(jnp.concatenate([mpack, gap, lpack, gap], axis=0))[0:ns, :]
-    lane_s = lax.broadcasted_iota(I32, (sb, LANES), 1)
-    half = LANES // 2
-    for ct in range(cores):
-        part = mlt[ct * sb : (ct + 1) * sb, :]
-        for cx in range(nx):
-            s1m[ct * nx + cx] = part if cx == 0 else pltpu.roll(part, LANES - cx * hq, 1)
-            for j in range(hq):
-                s1[ct * nx + cx, j] = ofin[ct * sb : (ct + 1) * sb, cx * hq + j, :].astype(BF16)
-    r1[t * nx + x] = s1[t * nx + x]
-    r1m[t * nx + x] = s1m[t * nx + x]
-
-    pl.semaphore_wait(barrier, len(xpeers) + jnp.where(z == spots[0], nx, jnp.where(z == spots[1], 1, cores)))
-
-    for px, pt in xpeers:
-        remote(s1.at[pt * nx + px], r1.at[t * nx + x], s1s_sem, s1r_sem, at(px, z, pt)).start()
-        remote(s1m.at[pt * nx + px], r1m.at[t * nx + x], m1s_sem, m1r_sem, at(px, z, pt)).start()
+        ml = jnp.where(lane_h == s, mrun[f], ml)
+        ml = jnp.where(lane_h == half + s, lrun[f], ml)
+    ml_a = ml.astype(BF16).astype(F32)
+    ml_b = (ml - ml_a).astype(BF16).astype(F32)
+    ml_c = ml - ml_a - ml_b
+    none = jnp.zeros((hh, LANES), F32)
+    for cx in range(nx):
+        for cp in range(2):
+            h0 = cx * hq + cp * hh
+            tail = jnp.concatenate(
+                [ml_a[h0 : h0 + hh], ml_b[h0 : h0 + hh], ml_c[h0 : h0 + hh], none], axis=0).astype(BF16)
+            for ct in range(cores):
+                d = (cx * 2 + cp) * cores + ct
+                s1[d, hh] = tail[: 2 * hh]
+                s1[d, hh + 1] = tail[2 * hh :]
+                for j in range(hh):
+                    s1[d, j] = ofin[ct * sb : (ct + 1) * sb, h0 + j, :].astype(BF16)
+    here = (t * nx + x) * 2 + zp
+    r1[here] = s1[(x * 2 + zp) * cores + t]
+
+    pl.semaphore_wait(barrier, len(peers) + jnp.where(z < 2, 0, 1))
+
+    for px, pp, pt in peers:
+        remote(s1.at[(px * 2 + pp) * cores + pt], r1.at[here], s1s_sem, s1r_sem, at(px, z - zp + pp, pt)).start()
 
     def bulk(ref, blocks, send, recv):
         part = ref.at[pl.ds(0, blocks)]
         return remote(part, part, send, recv, at(x, z, (t + 1) % cores))
 
-    bulk(r1m, len(xpeers), m1s_sem, m1r_sem).wait_recv()
-    bulk(r1, len(xpeers), s1s_sem, s1r_sem).wait_recv()
+    bulk(r1, len(peers), s1s_sem, s1r_sem).wait_recv()
+
+    hn = cores * hh
+    row_h = lax.broadcasted_iota(I32, (hn, LANES), 0)
+    lane_r = lax.broadcasted_iota(I32, (hn, LANES), 1)
 
     def merged(ml):
         top = functools.reduce(jnp.maximum, ml)
@@ -218,24 +228,40 @@
         tot = functools.reduce(jnp.add, [f * pltpu.roll(m, half, 1) for f, m in zip(fs, ml)])
         return top, fs, tot
 
-    for o in reversed(range(cores)):
-        top, fs, tot = merged([r1m[o * nx + cx] for cx in range(nx)])
-        s2m[o] = jnp.where(lane_s < half, top, pltpu.roll(tot, half, 1))
-        for j in range(hq):
+    def as_columns(fs):
+        pad = jnp.zeros((LANES - len(fs) * hn, LANES), F32)
+        ft = jnp.transpose(jnp.concatenate(fs + [pad], axis=0))
+        return jnp.where(t == 0, ft[:sb], ft[sb : 2 * sb])
+
+    def source_ml(i):
+        both = []
+        for ct in range(cores):
+            k = ct * nx * 2 + i
+            y = r1[k, hh].astype(F32) + r1[k, hh + 1].astype(F32)
+            both.append(y + pltpu.roll(y, hh, 0))
+        return jnp.where(row_h < hh, both[0], both[1])
+
+    top, fs, tot = merged([source_ml(i) for i in range(nx * 2)])
+    s2m[...] = jnp.where(lane_r < half, top, pltpu.roll(tot, half, 1))
+    ft = as_columns(fs)
+    for ct in range(cores):
+        for j in range(hh):
+            k = ct * hh + j
             num = functools.reduce(
                 jnp.add,
-                [jnp.broadcast_to(fs[cx][:, j : j + 1], (sb, hd)) * r1[o * nx + cx, j].astype(F32) for cx in range(nx)])
-            s2[o, j] = num.astype(BF16)
-
-        @pl.when(z != spots[o])
-        def _():
-            remote(s2m.at[o], r2m.at[z], m2s_sem, m2r_sem, at(x, spots[o], t)).start()
-            remote(s2.at[o], r2.at[z], s2s_sem, s2r_sem, at(x, spots[o], t)).start()
-
-        @pl.when(z == spots[o])
-        def _():
-            r2[z] = s2[o]
-            r2m[z] = s2m[o]
+                [jnp.broadcast_to(ft[:, i * hn + k : i * hn + k + 1], (sb, hd)) * r1[ct * nx * 2 + i, j].astype(F32)
+                 for i in range(nx * 2)])
+            s2[k] = num.astype(BF16)
+
+    @pl.when(z >= 2)
+    def _():
+        remote(s2m, r2m.at[z // 2], m2s_sem, m2r_sem, at(x, zp, t)).start()
+        remote(s2, r2.at[z // 2], s2s_sem, s2r_sem, at(x, zp, t)).start()
+
+    @pl.when(z < 2)
+    def _():
+        r2[0] = s2[...]
+        r2m[0] = s2m[...]
 
     w_send = remote(w_v.at[t], w_v.at[t], ws_sem, wr_sem, at(x, z, (t + 1) % cores))
     w_recv = remote(w_v.at[t], w_v.at[(t + 1) % cores], ws_sem, wr_sem, at(x, z, (t + 1) % cores))
@@ -263,16 +289,17 @@
 
         @pl.when(z == spots[o])
         def _():
-            bulk(r2m, nz - 1, m2s_sem, m2r_sem).wait_recv()
-            bulk(r2, nz - 1, s2s_sem, s2r_sem).wait_recv()
-            top, fs, tot = merged([r2m[i] for i in range(nz)])
-            inv = jnp.where(lane_s < hq, 1.0 / tot, 0.0)
-            fs = [f * inv for f in fs]
-            for j in range(hq):
+            bulk(r2m, nz // 2 - 1, m2s_sem, m2r_sem).wait_recv()
+            bulk(r2, nz // 2 - 1, s2s_sem, s2r_sem).wait_recv()
+            top, fs, tot = merged([r2m[i] for i in range(nz // 2)])
+            inv = jnp.where(lane_r < ns, 1.0 / tot, 0.0)
+            ft = as_columns([f * inv for f in fs])
+            for k in range(hn):
                 att = functools.reduce(
                     jnp.add,
-                    [jnp.broadcast_to(fs[i][:, j : j + 1], (sb, hd)) * r2[i, j].astype(F32) for i in range(nz)])
-                g_v[x, o, j] = att.astype(BF16)
+                    [jnp.broadcast_to(ft[:, i * hn + k : i * hn + k + 1], (sb, hd)) * r2[i, k].astype(F32)
+                     for i in range(nz // 2)])
+                g_v[x, o, k] = att.astype(BF16)
             if o == 0:
                 for dx in xorder + [0]:
                     direct(dx).start()
@@ -299,7 +326,7 @@
     w_recv.wait_recv()
 
     def bytes_of(blocks, send, recv):
-        part = k_v.at[pl.ds(0, blocks * hq * sb)]
+        part = k_v.at[pl.ds(0, blocks * hn * sb)]
         return remote(part, part, send, recv, at(x, z, (t + 1) % cores))
 
     out = jnp.zeros((sb, hd), F32)
@@ -309,25 +336,20 @@
                 bytes_of(nx - 1, gxs_sem, peer_sem.at[o]).wait_recv()
             for dx in [0] if mine else xorder:
                 sx = (x + dx) % nx
-                for j in range(0, hq, 2):
-                    lhs = jnp.concatenate([g_v[sx, o, j], g_v[sx, o, j + 1]], axis=1)
-                    first = pl.multiple_of((sx * hq + j) * hd, 2 * hd)
-                    out = out + jnp.dot(lhs, w_v[o, pl.ds(first, 2 * hd), :], preferred_element_type=F32)
+                for k in range(0, hn, 2):
+                    lhs = jnp.concatenate([g_v[sx, o, k], g_v[sx, o, k + 1]], axis=1)
+                    head = sx * hq + (1 - o) * hh + k % hh
+                    first = pl.multiple_of(head * hd, 2 * hd)
+                    out = out + jnp.dot(lhs, w_v[k // hh, pl.ds(first, 2 * hd), :], preferred_element_type=F32)
     out_ref[...] = out.astype(out_ref.dtype)
 
     w_send.wait_send()
-    bulk(s1, len(xpeers), s1s_sem, s1r_sem).wait_send()
-    bulk(s1m, len(xpeers), m1s_sem, m1r_sem).wait_send()
-
-    @pl.when((z != spots[0]) & (z != spots[1]))
-    def _():
-        bulk(s2, cores, s2s_sem, s2r_sem).wait_send()
-        bulk(s2m, cores, m2s_sem, m2r_sem).wait_send()
-
-    @pl.when((z == spots[0]) | (z == spots[1]))
-    def _():
-        bulk(s2, 1, s2s_sem, s2r_sem).wait_send()
-        bulk(s2m, 1, m2s_sem, m2r_sem).wait_send()
+    bulk(s1, len(peers), s1s_sem, s1r_sem).wait_send()
+
+    @pl.when(z >= 2)
+    def _():
+        remote(s2, s2, s2s_sem, s2r_sem, at(x, z, (t + 1) % cores)).wait_send()
+        remote(s2m, s2m, m2s_sem, m2r_sem, at(x, z, (t + 1) % cores)).wait_send()
 
     @pl.when(z == spots[0])
     def _():
@@ -349,7 +371,7 @@
     cores = lax.axis_size("tensor")
     nz = ns
     nx = lax.axis_size("seq") // nz
-    hq = hl // nx
+    hh = hl // nx // 2
     sb = ns // cores
     rows = page_len * kvh
     pr = page_order.shape[0] // LANES
@@ -380,17 +402,15 @@
             pltpu.VMEM((pages + 1, hl, LANES), F32),
             pltpu.VMEM((pages + 1, hl, hd), F32),
             pltpu.VMEM((ns, hl, hd), F32),
-            pltpu.VMEM((cores * nx, hq, sb, hd), BF16),
-            pltpu.VMEM((cores * nx, hq, sb, hd), BF16),
-            pltpu.VMEM((cores, hq, sb, hd), BF16),
-            pltpu.VMEM((nz, hq, sb, hd), BF16),
-            pltpu.VMEM((cores * nx, sb, LANES), F32),
-            pltpu.VMEM((cores * nx, sb, LANES), F32),
-            pltpu.VMEM((cores, sb, LANES), F32),
-            pltpu.VMEM((nz, sb, LANES), F32),
-            pltpu.VMEM((nx, cores, hq, sb, hd), BF16),
+            pltpu.VMEM((cores * nx * 2, hh + 2, sb, hd), BF16),
+            pltpu.VMEM((cores * nx * 2, hh + 2, sb, hd), BF16),
+            pltpu.VMEM((cores * hh, sb, hd), BF16),
+            pltpu.VMEM((nz // 2, cores * hh, sb, hd), BF16),
+            pltpu.VMEM((cores * hh, LANES), F32),
+            pltpu.VMEM((nz // 2, cores * hh, LANES), F32),
+            pltpu.VMEM((nx, 2, cores * hh, sb, hd), BF16),
             dma, dma, dma((steps,)), dma((steps,)), dma, dma, dma, dma, dma,
-            dma, dma, dma, dma, dma, dma, dma, dma, dma, dma, dma((cores,)), dma((cores,)),
+            dma, dma, dma, dma, dma, dma, dma, dma, dma((2,)), dma((2,)),
         ],
         compiler_params=pltpu.CompilerParams(collective_id=0, has_side_effects=True),
         name="paged_decode",

time: 46 us -> 43.6 us (0.948)
  Pallas kernels: 45 us -> 43 us
    pallas_call x1, Pallas kernels: 45 us -> 43 us  [body(): pl.pallas_call(functools.partial(kernel, dims), out_shape=pltpu.VMEM((sb,...]
where the time goes in v4:
time: 43.6 us; the launch traced here: 43.5 us
  Pallas kernels  43 us (99%)
  local copies, waits for them, and re-layouts  0.58 us (1%)
    pallas_call x1, Pallas kernels, body(): pl.pallas_call(functools.partial(kernel, dims), out_shape=pltpu.VMEM((sb,...  43 us

profile of v4, /device:TPU:40, one launch (start us, length us, event | category | flops | bytes accessed | tf_op | source)
XLA Modules:
  0.0 43.5 jit_solution(13564984647100715716)
XLA Ops:
  0.0 43.0 %paged_decode.1 = bf16[8,128]{1,0:T(8,128)(2,1)S(1)} custom-call(s32[16]{0:T(128)} %len_hbm.1, bf16[16,32,128]{2,1,0:T(8,128)(2,1)} %q_hbm.1, bf16[16384,128]{1,0:T(8,128)(2,1)} %bitcast.3, bf16[16384,128]{1,0:T(8,128)(2,1)} %bitcast.4, s32[16,128]{1,0:T(8,128)} %bitcast.5, bf16[4096,128]{1,0:T(8,128)(2,1)} %w_hbm.1), custom_call_target="tpu_custom_call" | custom-call | tf_op jit(solution)/shard_map/paged_decode/pallas_call | solution.py:382
  43.0 0.6 %copy.8 = bf16[8,128]{1,0:T(8,128)(2,1)} copy(bf16[8,128]{1,0:T(8,128)(2,1)S(1)} %paged_decode.1) | data formatting | bytes 4096

commit v5 on v4

--- a/solution.py
+++ b/solution.py
@@ -14,16 +14,17 @@
 I32 = jnp.int32
 LANES = 128
 NEG = -1e30
-PAGES_PER_STEP = 8
+K_PARTS = (12, 20)
+V_PARTS = (32,)
 
 
 def kernel(
     dims,
     len_hbm, q_hbm, k_hbm, v_hbm, po_hbm, w_hbm, out_ref,
     len_s, q_v, k_v, v_v, po_v, w_v, val_v, meta_v, meta_s, cmod_v,
-    wt_v, mtop, ltot, mrun, lrun, orun, ofin, s1, r1, s2, r2, s2m, r2m, g_v,
+    wt_v, mtop, ltot, mrun, lrun, orun, ofin, s1, r1, s2, r2, g_v,
     len_sem, q_sem, k_sem, v_sem, po_sem, w_sem, meta_sem, ws_sem, wr_sem,
-    s1s_sem, s1r_sem, s2s_sem, s2r_sem, m2s_sem, m2r_sem, gzs_sem, gxs_sem, own_sem, peer_sem,
+    s1s_sem, s1r_sem, s2s_sem, s2r_sem, gzs_sem, gxs_sem, own_sem, peer_sem,
 ):
     nx, nz, pages, page_len, kvh, ns, hl, hd, cores = dims
     rows = page_len * kvh
@@ -35,7 +36,6 @@
     t = lax.axis_index("tensor")
     x = me // nz
     z = me % nz
-    steps = pages // PAGES_PER_STEP
     spots = (1, 0)
     zp = z % 2
     hh = hq // 2
@@ -69,16 +69,19 @@
     for px, pp, pt in peers[:early_greets]:
         greet(px, z - zp + pp, pt)
 
-    step_rows = PAGES_PER_STEP * rows
-
-    def kv_copy(src, dst, sem, c):
-        part = pl.ds(c * step_rows, step_rows)
-        return pltpu.make_async_copy(src.at[part], dst.at[part], sem.at[c])
-
-    for c in range(steps):
-        kv_copy(k_hbm, k_v, k_sem, c).start()
-    for c in range(steps):
-        kv_copy(v_hbm, v_v, v_sem, c).start()
+    def kv_copies(src, dst, sem, shares):
+        copies, first = [], 0
+        for i, share in enumerate(shares):
+            count = pages * share // sum(shares)
+            part = pl.ds(first * rows, count * rows)
+            copies.append((pltpu.make_async_copy(src.at[part], dst.at[part], sem.at[i]), range(first, first + count)))
+            first += count
+        return copies
+
+    k_copies = kv_copies(k_hbm, k_v, k_sem, K_PARTS)
+    v_copies = kv_copies(v_hbm, v_v, v_sem, V_PARTS)
+    for copy, _ in k_copies + v_copies:
+        copy.start()
     w_copy = pltpu.make_async_copy(w_hbm, w_v.at[t], w_sem)
     w_copy.start()
 
@@ -141,12 +144,11 @@
     q_copy.wait()
 
     def page_part(p):
-        return pl.ds(pl.multiple_of(p * rows, rows), rows)
-
-    def score_step(c, carry):
-        kv_copy(k_hbm, k_v, k_sem, c).wait()
-        for i in range(PAGES_PER_STEP):
-            p = c * PAGES_PER_STEP + i
+        return pl.ds(p * rows, rows)
+
+    for copy, part in k_copies:
+        copy.wait()
+        for p in part:
             code = meta_s[0, p]
             nvalid = jnp.bitwise_and(code, 255) * kvh
             own = jnp.minimum(jnp.bitwise_and(lax.shift_right_logical(code, 8), 31), ns - 1)
@@ -161,14 +163,10 @@
             mtop[p] = top
             ltot[p] = jnp.broadcast_to(jnp.sum(wt, axis=1, keepdims=True), (hl, LANES))
             mrun[p + 1] = jnp.maximum(mrun[before], top)
-        return carry
-
-    lax.fori_loop(0, steps, score_step, 0)
-
-    def value_step(c, carry):
-        kv_copy(v_hbm, v_v, v_sem, c).wait()
-        for i in range(PAGES_PER_STEP):
-            p = c * PAGES_PER_STEP + i
+
+    for copy, part in v_copies:
+        copy.wait()
+        for p in part:
             code = meta_s[0, p]
             own = jnp.bitwise_and(lax.shift_right_logical(code, 8), 31)
             before = jnp.clip(lax.shift_right_logical(code, 13), 0, pages)
@@ -177,9 +175,6 @@
             fb = jnp.exp2((mtop[p] - mrun[final]) * scale)
             lrun[p + 1] = lrun[before] + fb * ltot[p]
             orun[p + 1] = orun[before] + fb * o
-        return carry
-
-    lax.fori_loop(0, steps, value_step, 0)
 
     lane_h = lax.broadcasted_iota(I32, (hl, LANES), 1)
     half = LANES // 2
@@ -189,19 +184,27 @@
         ofin[s] = orun[f]
         ml = jnp.where(lane_h == s, mrun[f], ml)
         ml = jnp.where(lane_h == half + s, lrun[f], ml)
-    ml_a = ml.astype(BF16).astype(F32)
-    ml_b = (ml - ml_a).astype(BF16).astype(F32)
-    ml_c = ml - ml_a - ml_b
-    none = jnp.zeros((hh, LANES), F32)
+    hn = cores * hh
+    row_h = lax.broadcasted_iota(I32, (hn, LANES), 0)
+    lane_r = lax.broadcasted_iota(I32, (hn, LANES), 1)
+
+    def split(v):
+        a = v.astype(BF16).astype(F32)
+        b = (v - a).astype(BF16).astype(F32)
+        return a + pltpu.roll(b, ns, 1) + pltpu.roll(v - a - b, 2 * ns, 1)
+
+    def joined(v):
+        return v + pltpu.roll(v, LANES - ns, 1) + pltpu.roll(v, LANES - 2 * ns, 1)
+
+    ml = split(ml)
     for cx in range(nx):
         for cp in range(2):
             h0 = cx * hq + cp * hh
-            tail = jnp.concatenate(
-                [ml_a[h0 : h0 + hh], ml_b[h0 : h0 + hh], ml_c[h0 : h0 + hh], none], axis=0).astype(BF16)
+            tail = jnp.concatenate([ml[h0 : h0 + hh]] * cores, axis=0)
+            tail = jnp.where(row_h // hh == t, tail, 0.0).astype(BF16)
             for ct in range(cores):
                 d = (cx * 2 + cp) * cores + ct
-                s1[d, hh] = tail[: 2 * hh]
-                s1[d, hh + 1] = tail[2 * hh :]
+                s1[d, hh] = tail
                 for j in range(hh):
                     s1[d, j] = ofin[ct * sb : (ct + 1) * sb, h0 + j, :].astype(BF16)
     here = (t * nx + x) * 2 + zp
@@ -217,10 +220,6 @@
         return remote(part, part, send, recv, at(x, z, (t + 1) % cores))
 
     bulk(r1, len(peers), s1s_sem, s1r_sem).wait_recv()
-
-    hn = cores * hh
-    row_h = lax.broadcasted_iota(I32, (hn, LANES), 0)
-    lane_r = lax.broadcasted_iota(I32, (hn, LANES), 1)
 
     def merged(ml):
         top = functools.reduce(jnp.maximum, ml)
@@ -234,15 +233,11 @@
         return jnp.where(t == 0, ft[:sb], ft[sb : 2 * sb])
 
     def source_ml(i):
-        both = []
-        for ct in range(cores):
-            k = ct * nx * 2 + i
-            y = r1[k, hh].astype(F32) + r1[k, hh + 1].astype(F32)
-            both.append(y + pltpu.roll(y, hh, 0))
-        return jnp.where(row_h < hh, both[0], both[1])
+        return joined(r1[i, hh].astype(F32) + r1[nx * 2 + i, hh].astype(F32))
 
     top, fs, tot = merged([source_ml(i) for i in range(nx * 2)])
-    s2m[...] = jnp.where(lane_r < half, top, pltpu.roll(tot, half, 1))
+    out_ml = jnp.where(lane_r < half, top, pltpu.roll(tot, half, 1))
+    s2[hn] = split(jnp.where(lane_r % half < ns, out_ml, 0.0)).astype(BF16)
     ft = as_columns(fs)
     for ct in range(cores):
         for j in range(hh):
@@ -255,13 +250,11 @@
 
     @pl.when(z >= 2)
     def _():
-        remote(s2m, r2m.at[z // 2], m2s_sem, m2r_sem, at(x, zp, t)).start()
         remote(s2, r2.at[z // 2], s2s_sem, s2r_sem, at(x, zp, t)).start()
 
     @pl.when(z < 2)
     def _():
         r2[0] = s2[...]
-        r2m[0] = s2m[...]
 
     w_send = remote(w_v.at[t], w_v.at[t], ws_sem, wr_sem, at(x, z, (t + 1) % cores))
     w_recv = remote(w_v.at[t], w_v.at[(t + 1) % cores], ws_sem, wr_sem, at(x, z, (t + 1) % cores))
@@ -289,9 +282,8 @@
 
         @pl.when(z == spots[o])
         def _():
-            bulk(r2m, nz // 2 - 1, m2s_sem, m2r_sem).wait_recv()
             bulk(r2, nz // 2 - 1, s2s_sem, s2r_sem).wait_recv()
-            top, fs, tot = merged([r2m[i] for i in range(nz // 2)])
+            top, fs, tot = merged([joined(r2[i, hn].astype(F32)) for i in range(nz // 2)])
             inv = jnp.where(lane_r < ns, 1.0 / tot, 0.0)
             ft = as_columns([f * inv for f in fs])
             for k in range(hn):
@@ -301,12 +293,13 @@
                      for i in range(nz // 2)])
                 g_v[x, o, k] = att.astype(BF16)
             if o == 0:
+                along_z(o, zorder[0]).start()
                 for dx in xorder + [0]:
                     direct(dx).start()
             else:
                 for dx in xorder:
                     along_x(o, dx).start()
-            for pz in zorder:
+            for pz in zorder[1 if o == 0 else 0 :]:
                 along_z(o, pz).start()
             if o == 0:
                 for dx in xorder:
@@ -349,7 +342,6 @@
     @pl.when(z >= 2)
     def _():
         remote(s2, s2, s2s_sem, s2r_sem, at(x, z, (t + 1) % cores)).wait_send()
-        remote(s2m, s2m, m2s_sem, m2r_sem, at(x, z, (t + 1) % cores)).wait_send()
 
     @pl.when(z == spots[0])
     def _():
@@ -377,7 +369,6 @@
     pr = page_order.shape[0] // LANES
     wr, wc = out_weight.shape
     dims = (nx, nz, pages, page_len, kvh, ns, hl, hd, cores)
-    steps = pages // PAGES_PER_STEP
     dma = pltpu.SemaphoreType.DMA
     return pl.pallas_call(
         functools.partial(kernel, dims),
@@ -402,15 +393,13 @@
             pltpu.VMEM((pages + 1, hl, LANES), F32),
             pltpu.VMEM((pages + 1, hl, hd), F32),
             pltpu.VMEM((ns, hl, hd), F32),
-            pltpu.VMEM((cores * nx * 2, hh + 2, sb, hd), BF16),
-            pltpu.VMEM((cores * nx * 2, hh + 2, sb, hd), BF16),
-            pltpu.VMEM((cores * hh, sb, hd), BF16),
-            pltpu.VMEM((nz // 2, cores * hh, sb, hd), BF16),
-            pltpu.VMEM((cores * hh, LANES), F32),
-            pltpu.VMEM((nz // 2, cores * hh, LANES), F32),
+            pltpu.VMEM((cores * nx * 2, hh + 1, sb, hd), BF16),
+            pltpu.VMEM((cores * nx * 2, hh + 1, sb, hd), BF16),
+            pltpu.VMEM((cores * hh + 1, sb, hd), BF16),
+            pltpu.VMEM((nz // 2, cores * hh + 1, sb, hd), BF16),
             pltpu.VMEM((nx, 2, cores * hh, sb, hd), BF16),
-            dma, dma, dma((steps,)), dma((steps,)), dma, dma, dma, dma, dma,
-            dma, dma, dma, dma, dma, dma, dma, dma, dma((2,)), dma((2,)),
+            dma, dma, dma((len(K_PARTS),)), dma((len(V_PARTS),)), dma, dma, dma, dma, dma,
+            dma, dma, dma, dma, dma, dma, dma((2,)), dma((2,)),
         ],
         compiler_params=pltpu.CompilerParams(collective_id=0, has_side_effects=True),
         name="paged_decode",

time: 43.6 us -> 42.2 us (0.968)
  Pallas kernels: 43 us -> 41.5 us
    pallas_call x1, Pallas kernels: 43 us -> 41.5 us  [body(): pl.pallas_call(functools.partial(kernel, dims), out_shape=pltpu.VMEM((sb,...]
where the time goes in v5:
time: 42.2 us; the launch traced here: 42.1 us
  Pallas kernels  41.5 us (98%)
  local copies, waits for them, and re-layouts  0.58 us (1%)
    pallas_call x1, Pallas kernels, body(): pl.pallas_call(functools.partial(kernel, dims), out_shape=pltpu.VMEM((sb,...  41.5 us

profile of v5, /device:TPU:40, one launch (start us, length us, event | category | flops | bytes accessed | tf_op | source)
XLA Modules:
  0.0 42.1 jit_solution(11150860525801272899)
XLA Ops:
  0.0 41.5 %paged_decode.1 = bf16[8,128]{1,0:T(8,128)(2,1)S(1)} custom-call(s32[16]{0:T(128)} %len_hbm.1, bf16[16,32,128]{2,1,0:T(8,128)(2,1)} %q_hbm.1, bf16[16384,128]{1,0:T(8,128)(2,1)} %bitcast.3, bf16[16384,128]{1,0:T(8,128)(2,1)} %bitcast.4, s32[16,128]{1,0:T(8,128)} %bitcast.5, bf16[4096,128]{1,0:T(8,128)(2,1)} %w_hbm.1), custom_call_target="tpu_custom_call" | custom-call | tf_op jit(solution)/shard_map/paged_decode/pallas_call | solution.py:373
  41.5 0.6 %copy.8 = bf16[8,128]{1,0:T(8,128)(2,1)} copy(bf16[8,128]{1,0:T(8,128)(2,1)S(1)} %paged_decode.1) | data formatting | bytes 4096

commit v6 on v5

--- a/solution.py
+++ b/solution.py
@@ -255,6 +255,12 @@
     @pl.when(z < 2)
     def _():
         r2[0] = s2[...]
+
+    bulk(s1, len(peers), s1s_sem, s1r_sem).wait_send()
+
+    @pl.when(z >= 2)
+    def _():
+        remote(s2, s2, s2s_sem, s2r_sem, at(x, z, (t + 1) % cores)).wait_send()
 
     w_send = remote(w_v.at[t], w_v.at[t], ws_sem, wr_sem, at(x, z, (t + 1) % cores))
     w_recv = remote(w_v.at[t], w_v.at[(t + 1) % cores], ws_sem, wr_sem, at(x, z, (t + 1) % cores))
@@ -312,10 +318,7 @@
             for dx in xorder:
                 along_x(o, dx).start()
 
-    @pl.when(z == spots[1])
-    def _():
-        own_arrival(0).wait_recv()
-
+    w_send.wait_send()
     w_recv.wait_recv()
 
     def bytes_of(blocks, send, recv):
@@ -323,25 +326,22 @@
         return remote(part, part, send, recv, at(x, z, (t + 1) % cores))
 
     out = jnp.zeros((sb, hd), F32)
-    for mine in (True, False):
-        for o in reversed(range(cores)):
-            if not mine:
+    for o in reversed(range(2)):
+        if o == 0:
+            @pl.when(z == spots[1])
+            def _():
+                own_arrival(0).wait_recv()
+
+        for dx in [0] + xorder:
+            if dx == xorder[0]:
                 bytes_of(nx - 1, gxs_sem, peer_sem.at[o]).wait_recv()
-            for dx in [0] if mine else xorder:
-                sx = (x + dx) % nx
-                for k in range(0, hn, 2):
-                    lhs = jnp.concatenate([g_v[sx, o, k], g_v[sx, o, k + 1]], axis=1)
-                    head = sx * hq + (1 - o) * hh + k % hh
-                    first = pl.multiple_of(head * hd, 2 * hd)
-                    out = out + jnp.dot(lhs, w_v[k // hh, pl.ds(first, 2 * hd), :], preferred_element_type=F32)
+            sx = (x + dx) % nx
+            for k in range(0, hn, 2):
+                lhs = jnp.concatenate([g_v[sx, o, k], g_v[sx, o, k + 1]], axis=1)
+                head = sx * hq + (1 - o) * hh + k % hh
+                first = pl.multiple_of(head * hd, 2 * hd)
+                out = out + jnp.dot(lhs, w_v[k // hh, pl.ds(first, 2 * hd), :], preferred_element_type=F32)
     out_ref[...] = out.astype(out_ref.dtype)
-
-    w_send.wait_send()
-    bulk(s1, len(peers), s1s_sem, s1r_sem).wait_send()
-
-    @pl.when(z >= 2)
-    def _():
-        remote(s2, s2, s2s_sem, s2r_sem, at(x, z, (t + 1) % cores)).wait_send()
 
     @pl.when(z == spots[0])
     def _():

time: 42.2 us -> 42.2 us (level)
  no operation moved by 1% of the time
where the time goes in v6:
time: 42.2 us; the launch traced here: 41.9 us
  Pallas kernels  41.3 us (98%)
  local copies, waits for them, and re-layouts  0.58 us (1%)
    pallas_call x1, Pallas kernels, body(): pl.pallas_call(functools.partial(kernel, dims), out_shape=pltpu.VMEM((sb,...  41.3 us

profile of v6, /device:TPU:40, one launch (start us, length us, event | category | flops | bytes accessed | tf_op | source)
XLA Modules:
  0.0 41.9 jit_solution(2120571274553934401)
XLA Ops:
  0.0 41.3 %paged_decode.1 = bf16[8,128]{1,0:T(8,128)(2,1)S(1)} custom-call(s32[16]{0:T(128)} %len_hbm.1, bf16[16,32,128]{2,1,0:T(8,128)(2,1)} %q_hbm.1, bf16[16384,128]{1,0:T(8,128)(2,1)} %bitcast.3, bf16[16384,128]{1,0:T(8,128)(2,1)} %bitcast.4, s32[16,128]{1,0:T(8,128)} %bitcast.5, bf16[4096,128]{1,0:T(8,128)(2,1)} %w_hbm.1), custom_call_target="tpu_custom_call" | custom-call | tf_op jit(solution)/shard_map/paged_decode/pallas_call | solution.py:373
  41.3 0.6 %copy.8 = bf16[8,128]{1,0:T(8,128)(2,1)} copy(bf16[8,128]{1,0:T(8,128)(2,1)S(1)} %paged_decode.1) | data formatting | bytes 4096

commit v7 on v6

--- a/solution.py
+++ b/solution.py
@@ -14,7 +14,7 @@
 I32 = jnp.int32
 LANES = 128
 NEG = -1e30
-K_PARTS = (12, 20)
+K_PARTS = (10, 22)
 V_PARTS = (32,)
 
 
@@ -298,14 +298,14 @@
                     [jnp.broadcast_to(ft[:, i * hn + k : i * hn + k + 1], (sb, hd)) * r2[i, k].astype(F32)
                      for i in range(nz // 2)])
                 g_v[x, o, k] = att.astype(BF16)
+            along_z(o, zorder[0]).start()
             if o == 0:
-                along_z(o, zorder[0]).start()
                 for dx in xorder + [0]:
                     direct(dx).start()
             else:
                 for dx in xorder:
                     along_x(o, dx).start()
-            for pz in zorder[1 if o == 0 else 0 :]:
+            for pz in zorder[1:]:
                 along_z(o, pz).start()
             if o == 0:
                 for dx in xorder:

time: 42.2 us -> 42.2 us (level)
  no operation moved by 1% of the time
where the time goes in v7:
time: 42.2 us; the launch traced here: 41.9 us
  Pallas kernels  41.3 us (98%)
  local copies, waits for them, and re-layouts  0.58 us (1%)
    pallas_call x1, Pallas kernels, body(): pl.pallas_call(functools.partial(kernel, dims), out_shape=pltpu.VMEM((sb,...  41.3 us

profile of v7, /device:TPU:40, one launch (start us, length us, event | category | flops | bytes accessed | tf_op | source)
XLA Modules:
  0.0 41.9 jit_solution(5934227350092900628)
XLA Ops:
  0.0 41.3 %paged_decode.1 = bf16[8,128]{1,0:T(8,128)(2,1)S(1)} custom-call(s32[16]{0:T(128)} %len_hbm.1, bf16[16,32,128]{2,1,0:T(8,128)(2,1)} %q_hbm.1, bf16[16384,128]{1,0:T(8,128)(2,1)} %bitcast.3, bf16[16384,128]{1,0:T(8,128)(2,1)} %bitcast.4, s32[16,128]{1,0:T(8,128)} %bitcast.5, bf16[4096,128]{1,0:T(8,128)(2,1)} %w_hbm.1), custom_call_target="tpu_custom_call" | custom-call | tf_op jit(solution)/shard_map/paged_decode/pallas_call | solution.py:373
  41.3 0.6 %copy.8 = bf16[8,128]{1,0:T(8,128)(2,1)} copy(bf16[8,128]{1,0:T(8,128)(2,1)S(1)} %paged_decode.1) | data formatting | bytes 4096
